TPU v7x, 256 devices: a whole 4x4x8 slice. The times are simulated.
256 devices in a mesh: space: 4 (over y_hi, core), shard: 64 (over x, z, y_lo).
Axes of the slice: x: 4, y: 4 (y_hi: 2, y_lo: 2; y = y_hi * 2 + y_lo), z: 8, core: 2. Of those that a mesh axis runs over, the one named last changes fastest.
Arguments:
- volume_field: float32 [2, 16, 16, 1024, 128], P(None, None, 'space', 'shard'), may hold values from -6 to 6
- source: float32 [2, 16, 16, 1024, 128], P(None, None, 'space', 'shard'), may hold values from -6 to 6
- material: int32 [16, 1024, 128], P('space', 'shard'), may hold values from 0 to 7
- mat_real: float32 [8], replicated, may hold values from 0.5 to 4
- mat_loss: float32 [8], replicated, may hold values from 0.1 to 1.5
- surface_map: int32 [4096, 128], P(('space', 'shard')), may hold values from 0 to 8191
- near_boxes: int32 [4096, 4], P(('space', 'shard')), may hold values from 0 to 4095, as said below
- near_blocks: bfloat16 [4, 256, 256], replicated, may hold values from -0.1875 to 0.1875
- radiate: bfloat16 [2, 128, 512], replicated, may hold values from -0.375 to 0.375
- interp: bfloat16 [512, 2048], replicated, may hold values from -0.25 to 0.25
- phase_angle: float32 [8, 2048], replicated, may hold values from -3.140625 to 3.140625
- far_parents: int32 [512, 8], replicated, may hold values from 0 to 511
- far_kind: int32 [512, 8], replicated, may hold values from 0 to 315
- translate: float32 [316, 2, 2048], P(None, None, 'shard'), may hold values from -0.18 to 0.18
Outputs:
- volume_out: float32 [2, 16, 16, 1024, 128], P(None, None, 'space', 'shard')
- forcing: float32 [4096, 16, 256], P(('space', 'shard'))
Inputs may be any that keep to these rules, and one draw needn't show every extreme that they name: near_boxes[b, 0] = b; every other entry is a box of the same group of 1024 boxes (boxes g * 1024 to (g + 1) * 1024 - 1) whose index lies from 16 below to 31 above the first box of b's run of 16 boxes.
All inputs are finite; a program needn't handle non-finite values.
Results may differ from a plain program's by a relative error of at most 0.015.
Values may be sent and summed in bfloat16 or wider, within the bound.
A program may use at most 128 MiB of HBM per device.

v0:
```python
import math

import jax
import jax.numpy as jnp
from jax import lax
from jax.sharding import PartitionSpec as P

relaxation = 0.8


def extended(array, sides, width):
    edges = {}
    for axis, dim in sides:
        peers, length = (lax.axis_size(axis), array.shape[dim])
        up = [(i, (i + 1) % peers) for i in range(peers - 1)]
        last = lax.slice_in_dim(array, length - width, length, axis=dim)
        leading = lax.slice_in_dim(array, 0, width, axis=dim)
        edges[dim] = (
            lax.ppermute(last, axis, up),
            lax.ppermute(leading, axis, [(b, a) for a, b in up]),
        )
    done = []
    for _, dim in sides:
        low, high = edges[dim]
        around = [(width, width) if d in done else (0, 0) for d in range(array.ndim)]
        array = jnp.concatenate([jnp.pad(low, around), array, jnp.pad(high, around)], axis=dim)
        done.append(dim)
    return array


def padded_2(array, sides, width):
    for axis, dim in sides:
        peers, length = (lax.axis_size(axis), array.shape[dim])
        up = [(i, (i + 1) % peers) for i in range(peers - 1)]
        down = [(j, i) for i, j in up]
        last = lax.slice_in_dim(array, length - width, length, axis=dim)
        leading = lax.slice_in_dim(array, 0, width, axis=dim)
        before = lax.ppermute(last, axis, up)
        after = lax.ppermute(leading, axis, down)
        array = jnp.concatenate([before, array, after], axis=dim)
    return array


def sent_to_all(array, axis):
    copies = jnp.broadcast_to(array, (lax.axis_size(axis), *array.shape))
    return lax.all_to_all(copies, axis, split_axis=0, concat_axis=0, tiled=True)


def joined_along(tiles, dim):
    tiles = jnp.moveaxis(tiles, 0, dim)
    lengths = tiles.shape
    return tiles.reshape(*lengths[:dim], lengths[dim] * lengths[dim + 1], *lengths[dim + 2 :])


def gathered_copies(array, axis, dim):
    tiles = sent_to_all(array, axis)
    return joined_along(tiles, dim)


def neighbour_sum(padded):
    core = padded[:, :, 1:-1, 1:-1]
    result = padded[:, :, 2:, 1:-1] + padded[:, :, :-2, 1:-1]
    result = result + padded[:, :, 1:-1, 2:] + padded[:, :, 1:-1, :-2]
    zero_layer = jnp.zeros(core.shape[:-1] + (1,), core.dtype)
    upper = jnp.concatenate([core[..., 1:], zero_layer], axis=-1)
    lower = jnp.concatenate([zero_layer, core[..., :-1]], axis=-1)
    return result + upper + lower


def relax_sweep(current, neighbours, source, diagonal_coef, loss_coef):
    real_part = diagonal_coef * current[0] - neighbours[0] - loss_coef * current[1]
    imag_part = diagonal_coef * current[1] - neighbours[1] + loss_coef * current[0]
    applied = jnp.stack([real_part, imag_part])
    return current + relaxation * (source - applied) / diagonal_coef


def block_matrix(radiate):
    upper = jnp.concatenate([radiate[0], radiate[1]], axis=1)
    lower = jnp.concatenate([-radiate[1], radiate[0]], axis=1)
    return jnp.concatenate([upper, lower], axis=0)


def aggregate(leaf_rows, interp, cosine, sine_part):
    parent_count = leaf_rows.shape[0] // 8
    excite = leaf_rows.shape[1]
    spread = jnp.dot(
        leaf_rows.reshape(-1, interp.shape[0]), interp, preferred_element_type=jnp.float32
    )
    spread = spread.reshape(parent_count, 8, excite, 2, interp.shape[1])
    cosine_wide = cosine[None, :, None, :]
    sine_wide = sine_part[None, :, None, :]
    real_part = jnp.sum(cosine_wide * spread[:, :, :, 0] - sine_wide * spread[:, :, :, 1], axis=1)
    imag_part = jnp.sum(sine_wide * spread[:, :, :, 0] + cosine_wide * spread[:, :, :, 1], axis=1)
    return jnp.stack([real_part, imag_part], axis=2).astype(jnp.bfloat16)


def combine_far(sources, table):
    real_table = table[:, :, None, 0]
    imag_table = table[:, :, None, 1]
    real_part = jnp.sum(real_table * sources[:, :, :, 0] - imag_table * sources[:, :, :, 1], axis=1)
    imag_part = jnp.sum(imag_table * sources[:, :, :, 0] + real_table * sources[:, :, :, 1], axis=1)
    return jnp.stack([real_part, imag_part], axis=2)


def disaggregate(incoming_rows, interp, cosine, sine_part, weights):
    parent_count = incoming_rows.shape[0]
    excite = incoming_rows.shape[1]
    widened = incoming_rows.astype(jnp.float32)[:, None]
    cosine_wide = cosine[None, :, None, :]
    sine_wide = sine_part[None, :, None, :]
    real_part = cosine_wide * widened[:, :, :, 0] + sine_wide * widened[:, :, :, 1]
    imag_part = cosine_wide * widened[:, :, :, 1] - sine_wide * widened[:, :, :, 0]
    shifted = jnp.stack([real_part, imag_part], axis=3).astype(jnp.bfloat16)
    leaf_in = jnp.dot(
        shifted.reshape(-1, interp.shape[1]), interp.T, preferred_element_type=jnp.float32
    ).astype(jnp.bfloat16)
    leaf_in = leaf_in.reshape(parent_count * 8 * excite, 2 * interp.shape[0])
    far_part = jnp.dot(leaf_in, weights.T, preferred_element_type=jnp.float32)
    return far_part.reshape(parent_count * 8, excite, weights.shape[0])


def select_cells(flat_field, cell_keys):
    cell_total = flat_field.shape[1]
    block_cells = math.gcd(cell_total, 1024)
    block_total = cell_total // block_cells
    positions = jnp.arange(block_cells, dtype=jnp.int32)

    def add_block(block_index, total):
        first = block_index * block_cells
        piece = lax.dynamic_slice_in_dim(flat_field, first, block_cells, 1)
        selector = (cell_keys[None, :] == (first + positions)[:, None]).astype(jnp.bfloat16)
        return total + jnp.dot(piece, selector, preferred_element_type=jnp.float32)

    empty = jnp.zeros((flat_field.shape[0], cell_keys.shape[0]), jnp.float32)
    return lax.fori_loop(0, block_total, add_block, empty)


def shards(
    volume_field,
    source,
    material,
    mat_real,
    mat_loss,
    surface_map,
    near_boxes,
    near_blocks,
    radiate,
    interp,
    phase_angle,
    far_parents,
    far_kind,
    translate,
):
    excite = volume_field.shape[1]
    cells_x = volume_field.shape[2]
    cells_y = volume_field.shape[3]
    cells_z = volume_field.shape[4]
    diagonal_coef = jnp.full(material.shape, 6.0, jnp.float32)
    loss_coef = jnp.zeros(material.shape, jnp.float32)
    for material_kind in range(mat_real.shape[0]):
        present = material == material_kind
        diagonal_coef = diagonal_coef + jnp.where(present, mat_real[material_kind], 0.0)
        loss_coef = loss_coef + jnp.where(present, mat_loss[material_kind], 0.0)
    current = volume_field
    for sweep_index in range(2):
        padded = extended(current.astype(jnp.bfloat16), (("space", 2), ("shard", 3)), 1).astype(
            current.dtype
        )
        current = relax_sweep(current, neighbour_sum(padded), source, diagonal_coef, loss_coef)
    box_count = surface_map.shape[0]
    unknowns = surface_map.shape[1]
    flat_field = current.reshape(2 * excite, cells_x * cells_y * cells_z).astype(jnp.bfloat16)
    sampled = select_cells(flat_field, surface_map.reshape(-1)).astype(jnp.bfloat16)
    sampled = sampled.reshape(2, excite, box_count, unknowns)
    currents = jnp.transpose(sampled, (2, 1, 0, 3)).reshape(box_count, excite, 2 * unknowns)
    device_rank = lax.axis_index("space") * lax.axis_size("shard") + lax.axis_index("shard")
    beside_all = padded_2(currents, (("shard", 0),), box_count)
    local_near = near_boxes - (device_rank * box_count - box_count)
    near_force = jnp.zeros((box_count, excite, 2 * unknowns), jnp.float32)
    for slot_index in range(near_boxes.shape[1]):
        picked = jnp.take(beside_all, local_near[:, slot_index], axis=0).reshape(
            box_count * excite, 2 * unknowns
        )
        near_force = near_force + jnp.dot(
            picked, near_blocks[slot_index], preferred_element_type=jnp.float32
        ).reshape(box_count, excite, 2 * unknowns)
    weights = block_matrix(radiate)
    leaf_dirs = interp.shape[0]
    leaf = jnp.dot(
        currents.reshape(box_count * excite, 2 * unknowns),
        weights,
        preferred_element_type=jnp.float32,
    ).astype(jnp.bfloat16)
    leaf = leaf.reshape(box_count, excite, 2, leaf_dirs)
    cosine = jnp.cos(phase_angle)
    sine_part = jnp.sin(phase_angle)
    parent_patterns = aggregate(leaf, interp, cosine, sine_part)
    directed = lax.all_to_all(parent_patterns, "shard", split_axis=3, concat_axis=0, tiled=True)
    group_parents = directed.shape[0]
    group_index = lax.axis_index("space")
    target_ids = lax.dynamic_slice_in_dim(
        far_parents, group_index * group_parents, group_parents, 0
    )
    target_kinds = lax.dynamic_slice_in_dim(far_kind, group_index * group_parents, group_parents, 0)
    table = jnp.take(translate, target_kinds, axis=0)
    gathered = gathered_copies(directed, "space", 0)
    sources = jnp.take(gathered, target_ids, axis=0).astype(jnp.float32)
    incoming = combine_far(sources, table).astype(jnp.bfloat16)
    far_force = disaggregate(
        lax.all_to_all(incoming, "shard", split_axis=0, concat_axis=3, tiled=True),
        interp,
        cosine,
        sine_part,
        weights,
    )
    forcing = near_force + far_force
    return (current, forcing)


def solution(mesh):
    return jax.shard_map(
        shards,
        mesh=mesh,
        in_specs=(
            P(None, None, "space", "shard", None),
            P(None, None, "space", "shard", None),
            P("space", "shard", None),
            P(),
            P(),
            P(("space", "shard"), None),
            P(("space", "shard"), None),
            P(),
            P(),
            P(),
            P(),
            P(),
            P(),
            P(None, None, "shard"),
        ),
        out_specs=(P(None, None, "space", "shard", None), P(("space", "shard"), None, None)),
        check_vma=False,
    )
```

profile of v0, /device:TPU:1, one launch (start us, length us, event | category | flops | bytes accessed | tf_op | source)
XLA Modules:
  0.0 238.4 jit_solution(12585446366366786209)
XLA Ops:
  4.2 4.6 %collective-permute-start = (bf16[2,16,4,1,128]{4,3,2,1,0:T(2,128)(2,1)S(1)}, bf16[2,16,4,1,128]{4,3,2,1,0:T(2,128)(2,1)S(1)}, u32[]{:S(2)}, u32[]{:S(2)}) collective-permute-start(bf16[2,16,4,1,128]{4,3,2,1,0:T(2,128)(2,1)S(1)} %get-tuple-element.172), channel_id=1, source_target_pairs={{0,1},{1,2},{2,3},{3,4},{4,5},{5,6},{6,7},{7,8},{8,9},{9,10},{10,1... | collective-permute-start | bytes 98312 | tf_op jit(solution)/shard_map/ppermute | solution.py:19
  8.9 5.0 %collective-permute-start.2 = (bf16[2,16,1,16,128]{4,3,2,1,0:T(8,128)(2,1)S(1)}, bf16[2,16,1,16,128]{4,3,2,1,0:T(8,128)(2,1)S(1)}, u32[]{:S(2)}, u32[]{:S(2)}) collective-permute-start(bf16[2,16,1,16,128]{4,3,2,1,0:T(8,128)(2,1)S(1)} %get-tuple-element.171), channel_id=1, source_target_pairs={{64,0},{128,64},{192,128},{65,1},{129,65},{193,129},{66,2},{130,66... | collective-permute-start | bytes 393224 | tf_op jit(solution)/shard_map/ppermute | solution.py:20
  13.9 3.0 %collective-permute-start.1 = (bf16[2,16,1,16,128]{4,3,2,1,0:T(8,128)(2,1)S(1)}, bf16[2,16,1,16,128]{4,3,2,1,0:T(8,128)(2,1)S(1)}, u32[]{:S(2)}, u32[]{:S(2)}) collective-permute-start(bf16[2,16,1,16,128]{4,3,2,1,0:T(8,128)(2,1)S(1)} %get-tuple-element.170), channel_id=1, source_target_pairs={{0,64},{64,128},{128,192},{1,65},{65,129},{129,193},{2,66},{66,130... | collective-permute-start | bytes 393224 | tf_op jit(solution)/shard_map/ppermute | solution.py:19
  21.7 5.2 %select_add_fusion.1 = (f32[4,16,128]{2,1,0:T(8,128)S(1)}, pred[4,16,128]{2,1,0:T(8,128)(4,1)S(1)}, pred[4,16,128]{2,1,0:T(8,128)(4,1)S(1)}, pred[4,16,128]{2,1,...) fusion(f32[]{:T(128)} %bitcast.7, f32[]{:T(128)} %bitcast.6, ...), kind=kLoop, calls=%fused_computation.118 | loop fusion | flops 196608 | bytes 131104 | tf_op jit(solution)/shard_map/add | solution.py:162
  26.9 5.0 %select_add_fusion = f32[4,16,128]{2,1,0:T(8,128)S(1)} fusion(pred[4,16,128]{2,1,0:T(8,128)(4,1)S(1)} %get-tuple-element.151, pred[4,16,128]{2,1,0:T(8,128)(4,1)S(1)} %get-tuple-element.150, pred[4,16,128]{2,1,0:T(8,128)(4,1)S(1)} %get-tuple-element.149, pred[4,16,128]{2,1,0:T(8,128)(4,1)S(1)} %get-tuple-element.148, ...), kind=kLoop, calls=%fused_computation.117 | loop fusion | flops 122880 | bytes 98336 | tf_op jit(solution)/shard_map/add | solution.py:163
  38.1 4.6 %collective-permute-start.4 = (bf16[2,16,4,1,128]{4,3,2,1,0:T(2,128)(2,1)}, bf16[2,16,4,1,128]{4,3,2,1,0:T(2,128)(2,1)}, u32[]{:S(2)}, u32[]{:S(2)}) collective-permute-start(bf16[2,16,4,1,128]{4,3,2,1,0:T(2,128)(2,1)} %get-tuple-element.168), channel_id=1, source_target_pairs={{0,1},{1,2},{2,3},{3,4},{4,5},{5,6},{6,7},{7,8},{8,9},{9,10},{10,1... | collective-permute-start | bytes 98312 | tf_op jit(solution)/shard_map/ppermute | solution.py:19
  42.7 1.9 collective-permute-start.6
  44.6 5.3 %collective-permute-start.5 = (bf16[2,16,1,16,128]{4,3,2,1,0:T(8,128)(2,1)}, bf16[2,16,1,16,128]{4,3,2,1,0:T(8,128)(2,1)}, u32[]{:S(2)}, u32[]{:S(2)}) collective-permute-start(bf16[2,16,1,16,128]{4,3,2,1,0:T(8,128)(2,1)} %get-tuple-element.166), channel_id=1, source_target_pairs={{0,64},{64,128},{128,192},{1,65},{65,129},{129,193},{2,66},{66,130... | collective-permute-start | bytes 393224 | tf_op jit(solution)/shard_map/ppermute | solution.py:19
  51.8 7.5 %gather_fusion = f32[1024,2,32]{2,1,0:T(2,128)} fusion(f32[316,2,32]{2,1,0:T(2,128)S(1)} %copy.108, s32[1024]{0:T(1024)S(1)} %broadcast_clamp_fusion.1), kind=kCustom, calls=%fused_computation.4 | custom fusion | bytes 528384 | tf_op jit(solution)/shard_map/jit(_take)/gather | solution.py:205
  59.3 1.8 fusion.23
  66.0 12.9 %while.14 = (s32[]{:T(128)}, f32[32,2048]{1,0:T(8,128)S(1)}, bf16[32,8192]{1,0:T(8,128)(2,1)S(1)}, s32[16,128]{1,0:T(8,128)S(1)}, s32[]{:T(128)}, /*index=5*/s32[]{:T(128)}, s32[]{:T(128)}, s32[]{:T(128)}) while((s32[]{:T(128)}, f32[32,2048]{1,0:T(8,128)S(1)}, bf16[32,8192]{1,0:T(8,128)(2,1)S(1)}, s32[16,128]{1,0:T(8,128)S(1)}, ...), condition=%wide.region_1.2_spmd.clone, body=%wide.region_0.1_spmd.clone.sunk | while | flops 136446976 | bytes 606365 | solution.py:135
  66.1 1.6 fusion.97
  67.7 1.6 fusion.97
  69.3 1.6 fusion.97
  70.9 1.6 fusion.97
  72.5 1.6 fusion.97
  74.1 1.6 fusion.97
  75.7 1.6 fusion.97
  77.3 1.6 fusion.97
  83.0 3.7 %copy.113 = bf16[2,16,2,2048]{1,2,0,3:T(2,128)(2,1)} copy(bf16[2,16,2,2048]{3,1,0,2:T(8,128)(2,1)S(1)} %pad_maximum_fusion.2) | data formatting | bytes 524288 | tf_op jit(solution)/shard_map/stack | solution.py:94
  86.6 7.3 %reshape.176 = bf16[64,2,1024]{2,1,0:T(2,128)(2,1)} reshape(bf16[2048,2,2,16]{3,2,1,0:T(2,128)(2,1)} %bitcast.144) | data formatting | bytes 524288
  94.0 16.2 %all-to-all-start = ((bf16[64,2,1024]{2,1,0:T(2,128)(2,1)}), bf16[64,2,1024]{2,1,0:T(2,128)(2,1)S(1)}, u32[]{:S(2)}, u32[]{:S(2)}) async-start(bf16[64,2,1024]{2,1,0:T(2,128)(2,1)} %reshape.176), calls=%async_computation | async-start | bytes 524288 | tf_op jit(solution)/shard_map/all_to_all | solution.py:198
  111.4 9.3 %all-to-all-done = bf16[64,2,1024]{2,1,0:T(2,128)(2,1)S(1)} async-done(((bf16[64,2,1024]{2,1,0:T(2,128)(2,1)}), bf16[64,2,1024]{2,1,0:T(2,128)(2,1)S(1)}, u32[]{:S(2)}, u32[]{:S(2)}) %all-to-all-start) | async-done | bytes 262176 | tf_op jit(solution)/shard_map/all_to_all | solution.py:198
  120.7 2.4 %reshape.177 = bf16[2048,2,2,16]{3,2,1,0:T(2,128)(2,1)} reshape(bf16[64,2,1024]{2,1,0:T(2,128)(2,1)S(1)} %all-to-all-done) | data formatting | bytes 524288
  123.1 5.0 %copy.126 = bf16[2,16,2,64,32]{4,1,2,0,3:T(8,128)(2,1)S(1)} copy(bf16[2,16,2,64,32]{1,2,0,4,3:T(2,128)(2,1)} %bitcast.145) | data formatting | bytes 524288 | tf_op jit(solution)/shard_map/all_to_all | solution.py:198
  130.5 3.5 %all-to-all-start.1 = ((bf16[4,128,16,2,32]{1,4,3,2,0:T(8,128)(2,1)}), bf16[4,128,16,2,32]{1,4,3,2,0:T(8,128)(2,1)S(1)}, u32[]{:S(2)}, u32[]{:S(2)}) async-start(bf16[4,128,16,2,32]{1,4,3,2,0:T(8,128)(2,1)} %broadcast_in_dim.151), calls=%async_computation.1 | async-start | bytes 2097152 | tf_op jit(solution)/shard_map/all_to_all | solution.py:46
  135.0 2.9 %collective-permute-start.8 = (bf16[16,16,256]{2,1,0:T(8,128)(2,1)S(1)}, bf16[16,16,256]{2,1,0:T(8,128)(2,1)S(1)}, u32[]{:S(2)}, u32[]{:S(2)}) collective-permute-start(bf16[16,16,256]{2,1,0:T(8,128)(2,1)S(1)} %reshape.102), channel_id=1, source_target_pairs={{0,1},{1,2},{2,3},{3,4},{4,5},{5,6},{6,7},{7,8},{8,9},{9,10},{10,1... | collective-permute-start | bytes 393224 | tf_op jit(solution)/shard_map/ppermute | solution.py:38
  139.3 12.0 %collective-permute-done.8 = bf16[16,16,256]{2,1,0:T(8,128)(2,1)S(1)} collective-permute-done((bf16[16,16,256]{2,1,0:T(8,128)(2,1)S(1)}, bf16[16,16,256]{2,1,0:T(8,128)(2,1)S(1)}, u32[]{:S(2)}, u32[]{:S(2)}) %collective-permute-start.8) | collective-permute-done | bytes 131104 | tf_op jit(solution)/shard_map/ppermute | solution.py:38
  153.3 2.2 gather_fusion.5
  155.5 6.4 %copy.117 = bf16[4,128,16,2,32]{4,2,3,1,0:T(8,128)(2,1)} copy(bf16[4,128,16,2,32]{1,4,3,2,0:T(8,128)(2,1)S(1)} %all-to-all-done.1) | data formatting | bytes 2097152 | tf_op jit(solution)/shard_map/all_to_all | solution.py:46
  161.9 12.0 %gather_fusion.1 = bf16[1024,16,2,32]{3,1,2,0:T(8,128)(2,1)} fusion(bf16[512,16,2,32]{3,1,2,0:T(8,128)(2,1)} %bitcast.142, s32[1024]{0:T(1024)S(1)} %broadcast_clamp_fusion), kind=kCustom, calls=%fused_computation.5 | custom fusion | bytes 4198400 | tf_op jit(solution)/shard_map/jit(_take)/gather | solution.py:207
  173.9 5.9 %fusion.11 = f32[128,8,16,2,32]{4,2,1,0,3:T(8,128)S(1)} fusion(bf16[128,8,16,2,32]{4,2,3,1,0:T(8,128)(2,1)} %bitcast.143, pred[128,8]{1,0:T(8,128)(4,1)S(1)} %copy.110), kind=kLoop, calls=%fused_computation.18 | loop fusion | flops 2097152 | bytes 6292480 | tf_op jit(solution)/shard_map/convert_element_type | solution.py:207
  179.9 3.8 %subtract_reduce_fusion = (bf16[128,16,32]{2,1,0:T(8,128)(2,1)S(1)}, bf16[128,16,32]{2,1,0:T(8,128)(2,1)S(1)}) fusion(f32[128,8,16,2,32]{4,2,1,0,3:T(8,128)S(1)} %fusion.11, f32[128,8,32]{2,1,0:T(8,128)S(1)} %copy-done.7, f32[128,8,32]{2,1,0:T(8,128)S(1)} %copy-done.6), kind=kLoop, calls=%fused_computation.20 | loop fusion | flops 4063232 | bytes 4718592 | tf_op jit(solution)/shard_map/reduce_sum | solution.py:100
  183.9 1.6 copy.120
  185.5 1.7 reshape.178
  187.2 7.5 %all-to-all-start.2 = ((bf16[64,2,1024]{2,1,0:T(2,128)(2,1)}), bf16[64,2,1024]{2,1,0:T(2,128)(2,1)S(1)}, u32[]{:S(2)}, u32[]{:S(2)}) async-start(bf16[64,2,1024]{2,1,0:T(2,128)(2,1)} %reshape.178), calls=%async_computation.2 | async-start | bytes 524288 | tf_op jit(solution)/shard_map/all_to_all | solution.py:210
  194.7 1.9 fusion.46
  199.7 2.2 gather_fusion.2
  202.0 1.8 fusion.48
  203.8 1.8 fusion.50
  207.0 2.5 %copy.122 = f32[128,16,2,32]{3,1,2,0:T(8,128)} copy(bf16[128,16,2,32]{0,3,2,1:T(8,128)(2,1)S(1)} %copy.121) | data formatting | bytes 786432 | tf_op jit(solution)/shard_map/convert_element_type | solution.py:108
  209.6 4.2 %copy.123 = f32[2,16,2,64,32]{4,3,1,2,0:T(8,128)} copy(f32[2,16,2,64,32]{4,1,2,0,3:T(8,128)} %bitcast.146) | data formatting | bytes 1048576 | tf_op jit(solution)/shard_map/convert_element_type | solution.py:108
  213.7 2.5 %reshape.104 = f32[2,1,16,2,2048]{4,2,3,0,1:T(8,128)S(1)} reshape(f32[2,16,2,64,32]{4,3,1,2,0:T(8,128)} %copy.123) | data formatting | bytes 1048576 | tf_op jit(solution)/shard_map/convert_element_type | solution.py:108
  216.3 4.4 %add_convert_fusion = (bf16[2,8,16,1,2048]{4,3,2,1,0:T(2,128)(2,1)S(1)}, bf16[2,8,16,1,2048]{4,3,2,1,0:T(2,128)(2,1)S(1)}) fusion(f32[2,16,2048]{2,1,0:T(8,128)S(1)} %get-tuple-element.165, f32[8,2048]{1,0:T(8,128)S(1)} %copy-done.13, f32[2,16,2048]{2,1,0:T(8,128)S(1)} %get-tuple-element.164, f32[8,2048]{1,0:T(8,128)S(1)} %copy-done.11), kind=kLoop, calls=%fused_computation.33 | loop fusion | flops 4194304 | bytes 2752512 | tf_op jit(solution)/shard_map/convert.3
  220.7 5.2 %pad_maximum_fusion = bf16[2,8,16,2,2048]{4,3,2,1,0:T(2,128)(2,1)} fusion(bf16[2,8,16,1,2048]{4,3,2,1,0:T(2,128)(2,1)S(1)} %get-tuple-element.163, bf16[2,8,16,1,2048]{4,3,2,1,0:T(2,128)(2,1)S(1)} %get-tuple-element.162), kind=kLoop, calls=%fused_computation.29 | loop fusion | flops 4194304 | bytes 4194304 | tf_op jit(solution)/shard_map/stack | solution.py:113
  226.0 4.1 %convert_element_type.77 = bf16[512,2048]{1,0:T(8,128)(2,1)} reshape(bf16[2,8,16,2,2048]{4,3,2,1,0:T(2,128)(2,1)} %pad_maximum_fusion) | data formatting | bytes 4194304 | tf_op jit(solution)/shard_map/convert_element_type | solution.py:113
  230.0 3.7 %convolution_convert_fusion = bf16[512,512]{1,0:T(8,128)(2,1)} fusion(bf16[512,2048]{1,0:T(8,128)(2,1)} %convert_element_type.77, bf16[512,2048]{1,0:T(8,128)(2,1)S(1)} %copy-done), kind=kOutput, calls=%fused_computation.36 | convolution fusion | flops 1074003968 | bytes 4718592 | tf_op jit(solution)/shard_map/dot_general | solution.py:114
  236.5 1.9 fusion.26
  (131 shorter events, 40.5 us)
Async XLA Ops:
  0.6 80.3 %copy-start = (bf16[512,2048]{1,0:T(8,128)(2,1)S(1)}, bf16[512,2048]{1,0:T(8,128)(2,1)}, u32[]{:S(2)}) copy-start(bf16[512,2048]{1,0:T(8,128)(2,1)} %param.27) | copy-start | bytes 6291460
  0.6 16.3 %copy-start.14 = (bf16[2,128,512]{2,1,0:T(8,128)(2,1)S(1)}, bf16[2,128,512]{2,1,0:T(8,128)(2,1)}, u32[]{:S(2)}) copy-start(bf16[2,128,512]{2,1,0:T(8,128)(2,1)} %param.26) | copy-start | bytes 786436
  0.7 17.7 %copy-start.20 = (f32[8]{0:T(128)S(1)}, f32[8]{0:T(128)}, u32[]{:S(2)}) copy-start(f32[8]{0:T(128)} %param.21) | copy-start | bytes 100
  0.7 18.3 %copy-start.21 = (f32[8]{0:T(128)S(1)}, f32[8]{0:T(128)}, u32[]{:S(2)}) copy-start(f32[8]{0:T(128)} %param.22) | copy-start | bytes 100
  0.7 19.0 %copy-start.19 = (f32[8,2048]{1,0:T(8,128)S(1)}, f32[8,2048]{1,0:T(8,128)}, u32[]{:S(2)}) copy-start(f32[8,2048]{1,0:T(8,128)} %param.28) | copy-start | bytes 196612
  0.7 21.0 %copy-start.22 = (s32[4,16,128]{2,1,0:T(8,128)S(1)}, s32[4,16,128]{2,1,0:T(8,128)}, u32[]{:S(2)}) copy-start(s32[4,16,128]{2,1,0:T(8,128)} %param.20) | copy-start | bytes 98308
  2.9 29.0 %collective-permute-start.3 = (bf16[2,16,4,1,128]{4,3,2,1,0:T(2,128)(2,1)}, bf16[2,16,4,1,128]{4,3,2,1,0:T(2,128)(2,1)S(1)}, u32[]{:S(2)}, u32[]{:S(2)}) collective-permute-start(bf16[2,16,4,1,128]{4,3,2,1,0:T(2,128)(2,1)} %get-tuple-element.173), channel_id=1, source_target_pairs={{1,0},{2,1},{3,2},{4,3},{5,4},{6,5},{7,6},{8,7},{9,8},{10,9},{11,1... | collective-permute-start | bytes 98312 | tf_op jit(solution)/shard_map/ppermute | solution.py:20
  4.2 27.7 %collective-permute-start = (bf16[2,16,4,1,128]{4,3,2,1,0:T(2,128)(2,1)S(1)}, bf16[2,16,4,1,128]{4,3,2,1,0:T(2,128)(2,1)S(1)}, u32[]{:S(2)}, u32[]{:S(2)}) collective-permute-start(bf16[2,16,4,1,128]{4,3,2,1,0:T(2,128)(2,1)S(1)} %get-tuple-element.172), channel_id=1, source_target_pairs={{0,1},{1,2},{2,3},{3,4},{4,5},{5,6},{6,7},{7,8},{8,9},{9,10},{10,1... | collective-permute-start | bytes 98312 | tf_op jit(solution)/shard_map/ppermute | solution.py:19
  8.9 23.1 %collective-permute-start.2 = (bf16[2,16,1,16,128]{4,3,2,1,0:T(8,128)(2,1)S(1)}, bf16[2,16,1,16,128]{4,3,2,1,0:T(8,128)(2,1)S(1)}, u32[]{:S(2)}, u32[]{:S(2)}) collective-permute-start(bf16[2,16,1,16,128]{4,3,2,1,0:T(8,128)(2,1)S(1)} %get-tuple-element.171), channel_id=1, source_target_pairs={{64,0},{128,64},{192,128},{65,1},{129,65},{193,129},{66,2},{130,66... | collective-permute-start | bytes 393224 | tf_op jit(solution)/shard_map/ppermute | solution.py:20
  13.9 18.1 %collective-permute-start.1 = (bf16[2,16,1,16,128]{4,3,2,1,0:T(8,128)(2,1)S(1)}, bf16[2,16,1,16,128]{4,3,2,1,0:T(8,128)(2,1)S(1)}, u32[]{:S(2)}, u32[]{:S(2)}) collective-permute-start(bf16[2,16,1,16,128]{4,3,2,1,0:T(8,128)(2,1)S(1)} %get-tuple-element.170), channel_id=1, source_target_pairs={{0,64},{64,128},{128,192},{1,65},{65,129},{129,193},{2,66},{66,130... | collective-permute-start | bytes 393224 | tf_op jit(solution)/shard_map/ppermute | solution.py:19
  33.0 1.2 copy-start.1
  33.6 1.3 copy-start.3
  34.9 15.0 %copy-start.23 = (s32[16,4]{0,1:T(4,128)S(1)}, s32[16,4]{0,1:T(4,128)}, u32[]{:S(2)}) copy-start(s32[16,4]{0,1:T(4,128)} %param.24) | copy-start | bytes 772
  35.2 0.8 copy-start.5
  36.8 22.5 %collective-permute-start.7 = (bf16[2,16,4,1,128]{4,3,2,1,0:T(2,128)(2,1)}, bf16[2,16,4,1,128]{4,3,2,1,0:T(2,128)(2,1)}, u32[]{:S(2)}, u32[]{:S(2)}) collective-permute-start(bf16[2,16,4,1,128]{4,3,2,1,0:T(2,128)(2,1)} %get-tuple-element.169), channel_id=1, source_target_pairs={{1,0},{2,1},{3,2},{4,3},{5,4},{6,5},{7,6},{8,7},{9,8},{10,9},{11,1... | collective-permute-start | bytes 98312 | tf_op jit(solution)/shard_map/ppermute | solution.py:20
  38.1 21.2 %collective-permute-start.4 = (bf16[2,16,4,1,128]{4,3,2,1,0:T(2,128)(2,1)}, bf16[2,16,4,1,128]{4,3,2,1,0:T(2,128)(2,1)}, u32[]{:S(2)}, u32[]{:S(2)}) collective-permute-start(bf16[2,16,4,1,128]{4,3,2,1,0:T(2,128)(2,1)} %get-tuple-element.168), channel_id=1, source_target_pairs={{0,1},{1,2},{2,3},{3,4},{4,5},{5,6},{6,7},{7,8},{8,9},{9,10},{10,1... | collective-permute-start | bytes 98312 | tf_op jit(solution)/shard_map/ppermute | solution.py:19
  42.7 16.6 %collective-permute-start.6 = (bf16[2,16,1,16,128]{4,3,2,1,0:T(8,128)(2,1)}, bf16[2,16,1,16,128]{4,3,2,1,0:T(8,128)(2,1)}, u32[]{:S(2)}, u32[]{:S(2)}) collective-permute-start(bf16[2,16,1,16,128]{4,3,2,1,0:T(8,128)(2,1)} %get-tuple-element.167), channel_id=1, source_target_pairs={{64,0},{128,64},{192,128},{65,1},{129,65},{193,129},{66,2},{130,66... | collective-permute-start | bytes 393224 | tf_op jit(solution)/shard_map/ppermute | solution.py:20
  44.6 14.7 %collective-permute-start.5 = (bf16[2,16,1,16,128]{4,3,2,1,0:T(8,128)(2,1)}, bf16[2,16,1,16,128]{4,3,2,1,0:T(8,128)(2,1)}, u32[]{:S(2)}, u32[]{:S(2)}) collective-permute-start(bf16[2,16,1,16,128]{4,3,2,1,0:T(8,128)(2,1)} %get-tuple-element.166), channel_id=1, source_target_pairs={{0,64},{64,128},{128,192},{1,65},{65,129},{129,193},{2,66},{66,130... | collective-permute-start | bytes 393224 | tf_op jit(solution)/shard_map/ppermute | solution.py:19
  62.0 1.2 copy-start.4
  63.2 2.8 %copy-start.17 = (f32[32,2048]{1,0:T(8,128)S(1)}, f32[32,2048]{1,0:T(8,128)}, u32[]{:S(2)}) copy-start(f32[32,2048]{1,0:T(8,128)} %custom-call) | copy-start | bytes 786436
  63.2 2.8 %copy-start.24 = (s32[16,128]{1,0:T(8,128)S(1)}, s32[16,128]{1,0:T(8,128)}, u32[]{:S(2)}) copy-start(s32[16,128]{1,0:T(8,128)} %param.23) | copy-start | bytes 24580
  79.1 3.1 %copy-start.16 = (bf16[2,16,16,128]{3,0,1,2:T(2,128)(2,1)}, bf16[2,16,16,128]{3,0,1,2:T(2,128)(2,1)S(1)}, u32[]{:S(2)}) copy-start(bf16[2,16,16,128]{3,0,1,2:T(2,128)(2,1)S(1)} %copy.142) | copy-start | bytes 393220
  81.0 1.3 copy-start.11
  81.0 1.3 copy-start.12
  82.9 27.2 %copy-start.2 = (f32[1024,2,32]{2,1,0:T(2,128)S(1)}, f32[1024,2,32]{2,1,0:T(2,128)}, u32[]{:S(2)}) copy-start(f32[1024,2,32]{2,1,0:T(2,128)} %gather_fusion) | copy-start | bytes 786436
  83.0 27.2 %copy-start.18 = (pred[128,8]{1,0:T(8,128)(4,1)S(1)}, pred[128,8]{1,0:T(8,128)(4,1)}, u32[]{:S(2)}) copy-start(pred[128,8]{1,0:T(8,128)(4,1)} %copy.106) | copy-start | bytes 3076
  94.0 26.8 %all-to-all-start = ((bf16[64,2,1024]{2,1,0:T(2,128)(2,1)}), bf16[64,2,1024]{2,1,0:T(2,128)(2,1)S(1)}, u32[]{:S(2)}, u32[]{:S(2)}) async-start(bf16[64,2,1024]{2,1,0:T(2,128)(2,1)} %reshape.176), calls=%async_computation | async-start | bytes 524288 | tf_op jit(solution)/shard_map/all_to_all | solution.py:198
  130.5 25.0 %all-to-all-start.1 = ((bf16[4,128,16,2,32]{1,4,3,2,0:T(8,128)(2,1)}), bf16[4,128,16,2,32]{1,4,3,2,0:T(8,128)(2,1)S(1)}, u32[]{:S(2)}, u32[]{:S(2)}) async-start(bf16[4,128,16,2,32]{1,4,3,2,0:T(8,128)(2,1)} %broadcast_in_dim.151), calls=%async_computation.1 | async-start | bytes 2097152 | tf_op jit(solution)/shard_map/all_to_all | solution.py:46
  135.0 16.3 %collective-permute-start.8 = (bf16[16,16,256]{2,1,0:T(8,128)(2,1)S(1)}, bf16[16,16,256]{2,1,0:T(8,128)(2,1)S(1)}, u32[]{:S(2)}, u32[]{:S(2)}) collective-permute-start(bf16[16,16,256]{2,1,0:T(8,128)(2,1)S(1)} %reshape.102), channel_id=1, source_target_pairs={{0,1},{1,2},{2,3},{3,4},{4,5},{5,6},{6,7},{7,8},{8,9},{9,10},{10,1... | collective-permute-start | bytes 393224 | tf_op jit(solution)/shard_map/ppermute | solution.py:38
  138.0 14.6 %collective-permute-start.9 = (bf16[16,16,256]{2,1,0:T(8,128)(2,1)S(1)}, bf16[16,16,256]{2,1,0:T(8,128)(2,1)S(1)}, u32[]{:S(2)}, u32[]{:S(2)}) collective-permute-start(bf16[16,16,256]{2,1,0:T(8,128)(2,1)S(1)} %reshape.102), channel_id=1, source_target_pairs={{1,0},{2,1},{3,2},{4,3},{5,4},{6,5},{7,6},{8,7},{9,8},{10,9},{11,1... | collective-permute-start | bytes 393224 | tf_op jit(solution)/shard_map/ppermute | solution.py:39
  173.9 5.9 %copy-start.6 = (f32[128,8,32]{2,1,0:T(8,128)S(1)}, f32[128,8,32]{2,1,0:T(8,128)}, u32[]{:S(2)}) copy-start(f32[128,8,32]{2,1,0:T(8,128)} %get-tuple-element.160) | copy-start | bytes 393220
  173.9 5.9 %copy-start.7 = (f32[128,8,32]{2,1,0:T(8,128)S(1)}, f32[128,8,32]{2,1,0:T(8,128)}, u32[]{:S(2)}) copy-start(f32[128,8,32]{2,1,0:T(8,128)} %get-tuple-element.161) | copy-start | bytes 393220
  187.2 18.4 %all-to-all-start.2 = ((bf16[64,2,1024]{2,1,0:T(2,128)(2,1)}), bf16[64,2,1024]{2,1,0:T(2,128)(2,1)S(1)}, u32[]{:S(2)}, u32[]{:S(2)}) async-start(bf16[64,2,1024]{2,1,0:T(2,128)(2,1)} %reshape.178), calls=%async_computation.2 | async-start | bytes 524288 | tf_op jit(solution)/shard_map/all_to_all | solution.py:210
  213.7 2.6 %copy-start.13 = (f32[8,2048]{1,0:T(8,128)S(1)}, f32[8,2048]{1,0:T(8,128)}, u32[]{:S(2)}) copy-start(f32[8,2048]{1,0:T(8,128)} %get-tuple-element.179) | copy-start | bytes 196612
  233.7 2.8 %copy-start.8 = (f32[16,16,256]{2,1,0:T(8,128)S(1)}, f32[16,16,256]{2,1,0:T(8,128)}, u32[]{:S(2)}) copy-start(f32[16,16,256]{2,1,0:T(8,128)} %fusion.46) | copy-start | bytes 786436
  233.7 2.8 %copy-start.9 = (f32[16,16,256]{2,1,0:T(8,128)S(1)}, f32[16,16,256]{2,1,0:T(8,128)}, u32[]{:S(2)}) copy-start(f32[16,16,256]{2,1,0:T(8,128)} %fusion.48) | copy-start | bytes 786436
  233.7 2.8 %copy-start.10 = (f32[16,16,256]{2,1,0:T(8,128)S(1)}, f32[16,16,256]{2,1,0:T(8,128)}, u32[]{:S(2)}) copy-start(f32[16,16,256]{2,1,0:T(8,128)} %fusion.50) | copy-start | bytes 786436
  233.7 2.8 %copy-start.15 = (bf16[16,16,256]{2,1,0:T(8,128)(2,1)S(1)}, bf16[16,16,256]{2,1,0:T(8,128)(2,1)}, u32[]{:S(2)}) copy-start(bf16[16,16,256]{2,1,0:T(8,128)(2,1)} %gather_fusion.2) | copy-start | bytes 393220
where the time goes:
time: 240 us; the launch traced here: 238 us
  local copies, waits for them, and re-layouts  89.8 us (37%)
  starting transfers between devices  58.4 us (24%)
  other arithmetic  39.3 us (16%)
  matrix products  27.8 us (12%)
  waiting for transfers between devices  21.3 us (9%)
    ppermute x4, starting transfers between devices, extended(): lax.ppermute(last, axis, up)  17.6 us
    unnamed x58, local copies, waits for them, and re-layouts  16.5 us
    all_to_all x1, starting transfers between devices, shards(): lax.all_to_all(parent_patterns, 'shard', split_axis=3, concat_axis=0, til...  16.2 us
    dot_general x8, matrix products, add_block(): return total + jnp.dot(piece, selector, preferred_element_type=jnp.float32)  12.5 us
    gather x1, local copies, waits for them, and re-layouts, shards(): sources = jnp.take(gathered, target_ids, axis=0).astype(jnp.float32)  12 us
    ppermute x1, waiting for transfers between devices, padded_2(): before = lax.ppermute(last, axis, up)  12 us
    ppermute x4, starting transfers between devices, extended(): lax.ppermute(leading, axis, [(b, a) for a, b in up])  9.48 us
    all_to_all x1, waiting for transfers between devices, shards(): lax.all_to_all(parent_patterns, 'shard', split_axis=3, concat_axis=0, til...  9.3 us
  transfers between devices with their start and end apart: 13, of which 2 were waited for; matrix products, arithmetic and copies ran while one was open for 18% of the time, Pallas kernels for 0%

commit v1 on v0

v1 whole, which is shorter than its diff:
```python
import jax
import jax.numpy as jnp
from jax import lax
from jax.experimental import pallas as pl
from jax.experimental.pallas import tpu as pltpu
from jax.sharding import PartitionSpec as P

MESH = pl.DeviceIdType.MESH
bf16 = jnp.bfloat16
f32 = jnp.float32
i32 = jnp.int32

relaxation = 0.8
SPACE = 4
SHARD = 64
DEVS = SPACE * SHARD
ROWS = 4
KB = 16
KINDS_PAD = 384


def dot(a, b):
    return jnp.dot(a, b, preferred_element_type=f32)


def neighbours(v, x_low, x_high, y_low, y_high):
    y = lax.broadcasted_iota(i32, (4, 16, 128), 1)
    z = lax.broadcasted_iota(i32, (4, 16, 128), 2)
    v4 = v.reshape(4, 16, 128)
    total = jnp.concatenate([v4[1:], x_high[None]], axis=0) + jnp.concatenate([x_low[None], v4[:3]], axis=0)
    down = pltpu.roll(v, 1, 0).reshape(4, 16, 128)
    total = total + jnp.where(y == 0, y_low[:, None, :], down)
    up = pltpu.roll(v, 63, 0).reshape(4, 16, 128)
    total = total + jnp.where(y == 15, y_high[:, None, :], up)
    total = total + jnp.where(z == 0, 0.0, pltpu.roll(v, 1, 1).reshape(4, 16, 128))
    total = total + jnp.where(z == 127, 0.0, pltpu.roll(v, 127, 1).reshape(4, 16, 128))
    return total.reshape(64, 128)


def kernel(
    vf_hbm, src_hbm, material, mat_real, mat_loss, surface, near_boxes, nb_hbm, rad_hbm, interp_hbm,
    phase, far_parents, far_kind, tr_hbm,
    vol_hbm, forcing,
    v0, v1, v2, src, interp, rad, nblk, tr,
    diag, loss, rinv,
    sx, sy, hx, hy, hyf,
    a_sel, oh_sel, n3, pick,
    m2, m2t, cosines, sines,
    oh_far, tt, tt_t, tg, pad,
    frows, pb, g, gg, acc, i2f, i2b, r, left, force,
    in_sem, halo_send, halo_recv, t_send, t_recv, near_send, near_recv, a_send, a_recv, self_sem, out_sem,
):
    space = lax.axis_index("space")
    shard = lax.axis_index("shard")
    me = space * SHARD + shard
    my_kb = shard // 4
    my_j = lax.rem(shard, 4)
    my_e = space * 4 + my_j

    barrier = pltpu.get_barrier_semaphore()

    def greet(i, carry):
        t = lax.rem(me + i, DEVS)
        pl.semaphore_signal(barrier, inc=1, device_id=(t // SHARD, lax.rem(t, SHARD)), device_id_type=MESH)
        return carry

    loads = [
        pltpu.make_async_copy(a, b, in_sem.at[n])
        for n, (a, b) in enumerate(
            [(vf_hbm, v0), (rad_hbm, rad), (interp_hbm, interp), (src_hbm, src), (tr_hbm, tr), (nb_hbm, nblk)]
        )
    ]
    for c in loads:
        c.start()
    lax.fori_loop(1, DEVS, greet, 0)

    mat = material[...].reshape(64, 128)
    d = jnp.full((64, 128), 6.0, f32)
    l = jnp.zeros((64, 128), f32)
    for m in range(8):
        here = mat == m
        d = d + jnp.where(here, mat_real[m], 0.0)
        l = l + jnp.where(here, mat_loss[m], 0.0)
    diag[...] = d
    loss[...] = l
    rinv[...] = relaxation / d

    loads[0].wait()
    for te in range(32):
        sx[0, 0, 16 * te : 16 * te + 16, :] = v0[64 * te : 64 * te + 16, :].astype(bf16)
        sx[0, 1, 16 * te : 16 * te + 16, :] = v0[64 * te + 48 : 64 * te + 64, :].astype(bf16)
    sy[0, 0] = v0[pl.ds(0, 128, stride=16), :].astype(bf16)
    sy[0, 1] = v0[pl.ds(15, 128, stride=16), :].astype(bf16)

    @pl.when(space == 0)
    def _():
        hx[0, 0] = jnp.zeros((512, 128), bf16)
        hx[1, 0] = jnp.zeros((512, 128), bf16)

    @pl.when(space == SPACE - 1)
    def _():
        hx[0, 1] = jnp.zeros((512, 128), bf16)
        hx[1, 1] = jnp.zeros((512, 128), bf16)

    @pl.when(shard == 0)
    def _():
        hy[0, 0] = jnp.zeros((128, 128), bf16)
        hy[1, 0] = jnp.zeros((128, 128), bf16)
        n3[0:16] = jnp.zeros((16, 16, 256), bf16)

    @pl.when(shard == SHARD - 1)
    def _():
        hy[0, 1] = jnp.zeros((128, 128), bf16)
        hy[1, 1] = jnp.zeros((128, 128), bf16)
        n3[32:48] = jnp.zeros((16, 16, 256), bf16)

    loads[1].wait()
    loads[2].wait()
    rad2 = rad[...].reshape(256, 512)

    def compose(kb, carry):
        cols = pl.multiple_of(kb * 128, 128)
        m = dot(rad2, interp[:, pl.ds(cols, 128)])
        m_re, m_im = m[:128], m[128:]
        both = jnp.concatenate(
            [jnp.concatenate([m_re, m_im], axis=1), jnp.concatenate([-m_im, m_re], axis=1)], axis=0
        )
        m2[kb] = both.astype(bf16)
        m2t[kb] = both.T.astype(bf16)
        angle = phase[:, pl.ds(cols, 128)]
        cosines[kb] = jnp.cos(angle)
        sines[kb] = jnp.sin(angle)
        return carry

    lax.fori_loop(0, KB, compose, 0)

    loads[4].wait()
    for c in range(2):
        pad[...] = jnp.zeros((KINDS_PAD, 128), f32)
        pad[0:316, 0:32] = tr[:, c, :]
        tt[c, pl.ds(pl.multiple_of(my_j * 32, 32), 32), :] = pad[...].T[0:32].astype(bf16)

    def select_hot(b, carry):
        cells = surface[pl.ds(b, 1), :]
        want = (cells // 2048) * 128 + lax.rem(cells, 128)
        rows = lax.broadcasted_iota(i32, (512, 128), 0)
        oh_sel[b] = jnp.where(rows == want, 1.0, 0.0).astype(bf16)
        return carry

    lax.fori_loop(0, 16, select_hot, 0)

    lanes = lax.broadcasted_iota(i32, (512, 512), 1)
    for f in range(8):
        oh_far[f] = jnp.where(far_parents[:, f : f + 1] == lanes, 1.0, 0.0).astype(bf16)

    loads[3].wait()
    pl.semaphore_wait(barrier, DEVS - 1)

    def copy_to(src_ref, dst_ref, send, recv, to):
        return pltpu.make_async_remote_copy(
            src_ref=src_ref, dst_ref=dst_ref, send_sem=send, recv_sem=recv, device_id=to, device_id_type=MESH
        )

    def halo_copies(w):
        return [
            (space > 0, copy_to(sx.at[w, 0], hx.at[w, 1], halo_send.at[w, 0], halo_recv.at[w, 1], (jnp.maximum(space - 1, 0), shard))),
            (space < SPACE - 1, copy_to(sx.at[w, 1], hx.at[w, 0], halo_send.at[w, 1], halo_recv.at[w, 0], (jnp.minimum(space + 1, SPACE - 1), shard))),
            (shard > 0, copy_to(sy.at[w, 0], hy.at[w, 1], halo_send.at[w, 2], halo_recv.at[w, 3], (space, jnp.maximum(shard - 1, 0)))),
            (shard < SHARD - 1, copy_to(sy.at[w, 1], hy.at[w, 0], halo_send.at[w, 3], halo_recv.at[w, 2], (space, jnp.minimum(shard + 1, SHARD - 1)))),
        ]

    def start_halo(w):
        for sent, c in halo_copies(w):
            pl.when(sent)(c.start)

    def wait_halo(w):
        copies = halo_copies(w)
        for k, other in ((0, 1), (1, 0), (2, 3), (3, 2)):
            pl.when(copies[other][0])(copies[k][1].wait_recv)
            pl.when(copies[k][0])(copies[k][1].wait_send)

    start_halo(0)

    def t_copy(step):
        rows = pl.ds(pl.multiple_of(my_j * 32, 32), 32)
        to = (space, my_kb * 4 + lax.rem(my_j + step, 4))
        return copy_to(tt.at[:, rows, :], tt.at[:, rows, :], t_send.at[step - 1], t_recv.at[step - 1], to)

    for step in (1, 2, 3):
        t_copy(step).start()

    def sweep(w, old, new):
        for side in range(2):
            hyf[side] = hy[w, side].astype(f32)

        def one(e, carry):
            parts = []
            for t in range(2):
                te = t * 16 + e
                rows = pl.ds(pl.multiple_of(te * 64, 64), 64)
                v = old[rows, :]
                xr = pl.ds(pl.multiple_of(te * 16, 16), 16)
                yr = pl.ds(pl.multiple_of(te * 4, 4), 4)
                near = neighbours(
                    v, hx[w, 0, xr, :].astype(f32), hx[w, 1, xr, :].astype(f32), hyf[0, yr, :], hyf[1, yr, :]
                )
                parts.append((te, rows, xr, v, near))
            dd, ll, rr = diag[...], loss[...], rinv[...]
            re, im = parts[0][3], parts[1][3]
            out_re = re + rr * (src[parts[0][1], :] - (dd * re - parts[0][4] - ll * im))
            out_im = im + rr * (src[parts[1][1], :] - (dd * im - parts[1][4] + ll * re))
            for (te, rows, xr, _, _), out in zip(parts, (out_re, out_im)):
                new[rows, :] = out
                narrow = out.astype(bf16)
                if w == 0:
                    sx[1, 0, xr, :] = narrow[0:16]
                    sx[1, 1, xr, :] = narrow[48:64]
                else:
                    for x in range(4):
                        a_sel[xr, 128 * x : 128 * x + 128] = narrow[16 * x : 16 * x + 16]
            return carry

        lax.fori_loop(0, 16, one, 0)

    wait_halo(0)
    sweep(0, v0, v1)
    sy[1, 0] = v1[pl.ds(0, 128, stride=16), :].astype(bf16)
    sy[1, 1] = v1[pl.ds(15, 128, stride=16), :].astype(bf16)
    start_halo(1)

    for step in (1, 2, 3):
        t_copy(step).wait_recv()
        t_copy(step).wait_send()
    for c in range(2):
        tt_t[:, 128 * c : 128 * c + 128] = tt[c].astype(f32).T.astype(bf16)
    kinds = lax.broadcasted_iota(i32, (512, KINDS_PAD), 1)
    for f in range(8):
        hot = jnp.where(far_kind[:, f : f + 1] == kinds, 1.0, 0.0).astype(bf16)
        tg[f] = dot(hot, tt_t[...])

    wait_halo(1)
    sweep(1, v1, v2)
    out_copy = pltpu.make_async_copy(v2, vol_hbm, out_sem.at[0])
    out_copy.start()

    def pick_box(b, carry):
        got = dot(a_sel[...], oh_sel[b])
        y = lax.rem(surface[pl.ds(b, 1), :] // 128, 16)
        keep = lax.broadcasted_iota(i32, (16, 128), 0) == y
        got = jnp.sum(jnp.where(keep[None], got.reshape(32, 16, 128), 0.0), axis=1).astype(bf16)
        n3[16 + b] = jnp.concatenate([got[:16], got[16:]], axis=1)
        return carry

    lax.fori_loop(0, 16, pick_box, 0)

    cur = n3[16:32].reshape(256, 256)

    def near_copies():
        return [
            (shard > 0, copy_to(n3.at[pl.ds(16, 16)], n3.at[pl.ds(32, 16)], near_send.at[0], near_recv.at[0], (space, jnp.maximum(shard - 1, 0)))),
            (shard < SHARD - 1, copy_to(n3.at[pl.ds(16, 16)], n3.at[pl.ds(0, 16)], near_send.at[1], near_recv.at[1], (space, jnp.minimum(shard + 1, SHARD - 1)))),
        ]

    def pattern(i):
        kb = lax.rem(my_kb + 1 + i, KB)
        spread = dot(cur, m2[kb])
        for p in range(2):
            re = jnp.zeros((16, 128), f32)
            im = jnp.zeros((16, 128), f32)
            for c in range(8):
                rows = spread[(p * 8 + c) * 16 : (p * 8 + c) * 16 + 16]
                s_re, s_im = rows[:, :128], rows[:, 128:]
                co, si = cosines[kb, c : c + 1, :], sines[kb, c : c + 1, :]
                re = re + (co * s_re - si * s_im)
                im = im + (si * s_re + co * s_im)
            frows[pl.ds(2 * p, 16, stride=4), :] = re
            frows[pl.ds(2 * p + 1, 16, stride=4), :] = im
        pb[pl.ds(pl.multiple_of(kb * 64, 64), 64), :] = frows[...].astype(bf16)

    def send_pattern(i):
        kb = lax.rem(my_kb + 1 + i, KB)

        def to_owner(j, carry):
            e = lax.rem(my_e + j, 16)
            to = (e // 4, kb * 4 + lax.rem(e, 4))
            from_rows = pl.ds(pl.multiple_of(kb * 64 + e * ROWS, ROWS), ROWS)
            to_rows = pl.ds(pl.multiple_of(me * ROWS, ROWS), ROWS)

            @pl.when(jnp.logical_or(kb != my_kb, e != my_e))
            def _():
                copy_to(pb.at[from_rows], g.at[to_rows], a_send.at[0], a_recv.at[0], to).start()

            return carry

        lax.fori_loop(0, 16, to_owner, 0)

    pattern(0)
    for sent, c in near_copies():
        pl.when(sent)(c.start)

    def step_out(i, carry):
        pattern(i)
        send_pattern(i - 1)
        return carry

    lax.fori_loop(1, KB, step_out, 0)
    send_pattern(KB - 1)
    my_rows = pl.ds(pl.multiple_of(me * ROWS, ROWS), ROWS)
    my_slot = pl.ds(pl.multiple_of((my_kb * 16 + my_e) * ROWS, ROWS), ROWS)
    own = pltpu.make_async_copy(pb.at[my_slot], g.at[my_rows], self_sem.at[0])
    own.start()

    sides = near_copies()
    pl.when(sides[1][0])(sides[0][1].wait_recv)
    pl.when(sides[0][0])(sides[1][1].wait_recv)
    for sent, c in sides:
        pl.when(sent)(c.wait_send)
    base = me * 16 - 16
    for s in range(4):
        for b in range(16):
            pick[16 * b : 16 * b + 16, 256 * s : 256 * s + 256] = n3[jnp.clip(near_boxes[b, s] - base, 0, 47)]
    loads[5].wait()
    force[...] = dot(pick[...], nblk[...].reshape(1024, 256))

    def wait_all(src_ref, dst_ref, k):
        count = pl.ds(0, (DEVS - 1) * ROWS)
        c = copy_to(src_ref.at[count], dst_ref.at[count], a_send.at[k], a_recv.at[k], (space, shard))
        c.wait_recv()
        c.wait_send()

    own.wait()
    wait_all(pb, g, 0)

    gg[:, 0:128] = g[pl.ds(0, 512, stride=2), :]
    gg[:, 128:256] = g[pl.ds(1, 512, stride=2), :]
    acc[...] = jnp.zeros((512, 256), f32)

    def far(f, carry):
        got = dot(oh_far[f], gg[...])
        t = tg[f]
        g_re, g_im, t_re, t_im = got[:, :128], got[:, 128:], t[:, :128], t[:, 128:]
        acc[:, 0:128] += t_re * g_re - t_im * g_im
        acc[:, 128:256] += t_im * g_re + t_re * g_im
        return carry

    lax.fori_loop(0, 8, far, 0)
    i2f[pl.ds(0, 512, stride=2), :] = acc[:, 0:128]
    i2f[pl.ds(1, 512, stride=2), :] = acc[:, 128:256]
    i2b[...] = i2f[...].astype(bf16)

    def back(i, carry):
        t = lax.rem(me + i, DEVS)
        rows = pl.ds(pl.multiple_of(t * ROWS, ROWS), ROWS)
        copy_to(i2b.at[rows], r.at[my_slot], a_send.at[1], a_recv.at[1], (t // SHARD, lax.rem(t, SHARD))).start()
        return carry

    lax.fori_loop(1, DEVS, back, 0)
    own_back = pltpu.make_async_copy(i2b.at[my_rows], r.at[my_slot], self_sem.at[1])
    own_back.start()
    own_back.wait()
    out_copy.wait()
    wait_all(i2b, r, 1)

    def bring(kb, carry):
        frows[...] = r[pl.ds(pl.multiple_of(kb * 64, 64), 64), :].astype(f32)
        for p in range(2):
            x_re = frows[pl.ds(2 * p, 16, stride=4), :]
            x_im = frows[pl.ds(2 * p + 1, 16, stride=4), :]
            for c in range(8):
                co, si = cosines[kb, c : c + 1, :], sines[kb, c : c + 1, :]
                at = (p * 8 + c) * 16
                left[at : at + 16, 0:128] = (co * x_re + si * x_im).astype(bf16)
                left[at : at + 16, 128:256] = (co * x_im - si * x_re).astype(bf16)
        force[...] += dot(left[...], m2t[kb])
        return carry

    lax.fori_loop(0, KB, bring, 0)
    forcing[...] = force[...]


def shards(
    volume_field, source, material, mat_real, mat_loss, surface_map, near_boxes, near_blocks, radiate, interp,
    phase_angle, far_parents, far_kind, translate,
):
    shape = volume_field.shape
    any_ = pl.BlockSpec(memory_space=pl.ANY)
    vmem = pl.BlockSpec(memory_space=pltpu.VMEM)
    smem = pl.BlockSpec(memory_space=pltpu.SMEM)
    V = pltpu.VMEM
    dma = pltpu.SemaphoreType.DMA
    volume, forcing = pl.pallas_call(
        kernel,
        out_shape=(jax.ShapeDtypeStruct((2048, 128), f32), jax.ShapeDtypeStruct((256, 256), f32)),
        in_specs=[any_, any_, vmem, smem, smem, vmem, smem, any_, any_, any_, vmem, vmem, vmem, any_],
        out_specs=(any_, vmem),
        scratch_shapes=[
            V((2048, 128), f32), V((2048, 128), f32), V((2048, 128), f32), V((2048, 128), f32),
            V((512, 2048), bf16), V((2, 128, 512), bf16), V((4, 256, 256), bf16), V((316, 2, 32), f32),
            V((64, 128), f32), V((64, 128), f32), V((64, 128), f32),
            V((2, 2, 512, 128), bf16), V((2, 2, 128, 128), bf16), V((2, 2, 512, 128), bf16), V((2, 2, 128, 128), bf16), V((2, 128, 128), f32),
            V((512, 512), bf16), V((16, 512, 128), bf16), V((48, 16, 256), bf16), V((256, 1024), bf16),
            V((16, 256, 256), bf16), V((16, 256, 256), bf16), V((16, 8, 128), f32), V((16, 8, 128), f32),
            V((8, 512, 512), bf16), V((2, 128, KINDS_PAD), bf16), V((KINDS_PAD, 256), bf16), V((8, 512, 256), f32), V((KINDS_PAD, 128), f32),
            V((64, 128), f32), V((1024, 128), bf16), V((1024, 128), bf16), V((512, 256), bf16), V((512, 256), f32),
            V((1024, 128), f32), V((1024, 128), bf16), V((1024, 128), bf16), V((256, 256), bf16), V((256, 256), f32),
            dma((6,)), dma((2, 4)), dma((2, 4)), dma((3,)), dma((3,)), dma((2,)), dma((2,)), dma((2,)), dma((2,)), dma((2,)), dma((1,)),
        ],
        compiler_params=pltpu.CompilerParams(collective_id=3, has_side_effects=True),
        name="relax_and_couple",
    )(
        volume_field.reshape(2048, 128), source.reshape(2048, 128), material, mat_real, mat_loss, surface_map,
        near_boxes, near_blocks, radiate, interp, phase_angle, far_parents, far_kind, translate,
    )
    return volume.reshape(shape), forcing.reshape(16, 16, 256)


def solution(mesh):
    return jax.shard_map(
        shards,
        mesh=mesh,
        in_specs=(
            P(None, None, "space", "shard", None),
            P(None, None, "space", "shard", None),
            P("space", "shard", None),
            P(),
            P(),
            P(("space", "shard"), None),
            P(("space", "shard"), None),
            P(),
            P(),
            P(),
            P(),
            P(),
            P(),
            P(None, None, "shard"),
        ),
        out_specs=(P(None, None, "space", "shard", None), P(("space", "shard"), None, None)),
        check_vma=False,
    )
```

time: 240 us -> 83.2 us (0.35)
  local copies, waits for them, and re-layouts: 89.8 us -> 9.32 us
  Pallas kernels: 0 us -> 72.9 us
  starting transfers between devices: 58.4 us -> 0 us
  other arithmetic: 39.3 us -> 0 us
  matrix products: 27.8 us -> 0 us
  waiting for transfers between devices: 21.3 us -> 0 us
    pallas_call x0 -> x1, Pallas kernels: none -> 72.9 us  [shards(): pl.pallas_call(kernel, out_shape=(jax.ShapeDtypeStruct((2048, 128), f32),...]
    ppermute x10 -> x0, starting transfers between devices: 31.3 us -> none  [the longest x4 17.6 us: extended(): lax.ppermute(last, axis, up)]
    dot_general x16 -> x0, matrix products: 27.8 us -> none  [the longest x8 12.5 us: add_block(): return total + jnp.dot(piece, selector, preferred_element_type=jnp.float32)]
    all_to_all x3 -> x0, starting transfers between devices: 27.1 us -> none  [the longest x1 16.2 us: shards(): lax.all_to_all(parent_patterns, 'shard', split_axis=3, concat_axis=0, til...]
    gather x6 -> x0, local copies, waits for them, and re-layouts: 27 us -> none  [the longest x1 12 us: shards(): sources = jnp.take(gathered, target_ids, axis=0).astype(jnp.float32)]
    convert_element_type x5 -> x0, local copies, waits for them, and re-layouts: 14.6 us -> none  [the longest x3 9.21 us: disaggregate(): widened = incoming_rows.astype(jnp.float32)[:, None]]
    all_to_all x4 -> x0, local copies, waits for them, and re-layouts: 13.3 us -> none  [the longest x1 6.4 us: sent_to_all(): return lax.all_to_all(copies, axis, split_axis=0, concat_axis=0, tiled=True)]
    ppermute x10 -> x0, waiting for transfers between devices: 12 us -> none  [the longest x1 12 us: padded_2(): before = lax.ppermute(last, axis, up)]
  transfers between devices with their start and end apart: 13 -> 0, of which waited for: 2 -> 0; matrix products, arithmetic and copies ran while one was open for 18% -> 0% of each run, Pallas kernels for 0% -> 0%
where the time goes in v1:
time: 83.2 us; the launch traced here: 82.9 us
  Pallas kernels  72.9 us (88%)
  local copies, waits for them, and re-layouts  9.32 us (11%)
    pallas_call x1, Pallas kernels, shards(): pl.pallas_call(kernel, out_shape=(jax.ShapeDtypeStruct((2048, 128), f32),...  72.9 us
    unnamed x8, local copies, waits for them, and re-layouts  9.32 us

profile of v1, /device:TPU:1, one launch (start us, length us, event | category | flops | bytes accessed | tf_op | source)
XLA Modules:
  0.0 82.9 jit_solution(13243611106545660100)
XLA Ops:
  0.6 1.4 %copy.16.near_boxes = s32[16,4]{1,0:T(8,128)} copy(s32[16,4]{0,1:T(4,128)} %param.20) | data formatting | bytes 512 | tf_op args[6]
  2.0 1.6 %copy.17.far_parents = s32[512,8]{1,0:T(8,128)} copy(s32[512,8]{0,1:T(8,128)} %param.25) | data formatting | bytes 32768 | tf_op args[11]
  3.5 1.6 %copy.18.far_kind = s32[512,8]{1,0:T(8,128)} copy(s32[512,8]{0,1:T(8,128)} %param.26) | data formatting | bytes 32768 | tf_op args[12]
  5.1 1.8 %copy.19.tr_hbm = f32[316,2,32]{2,1,0:T(2,128)} copy(f32[316,2,32]{0,2,1:T(8,128)} %param.27) | data formatting | bytes 161792 | tf_op args[13]
  6.9 72.9 %relax_and_couple.1 = (f32[2048,128]{1,0:T(8,128)}, f32[256,256]{1,0:T(8,128)}) custom-call(f32[2048,128]{1,0:T(8,128)} %bitcast.5, f32[2048,128]{1,0:T(8,128)} %bitcast.6, s32[4,16,128]{2,1,0:T(8,128)} %material.1, f32[8]{0:T(128)} %mat_real.1, f32[8]{0:T(128)} %mat_loss.1, s32[16,128]{1,0:T(8,128)} %surface.1, s32[16,4]{1,0:T(8,128)} %copy.16.near_boxes, ...), custom_call_target="tpu_custom_call" | custom-call | tf_op jit(solution)/shard_map/relax_and_couple/pallas_call | solution.py:391
  79.8 0.0 copy-start
  79.8 2.4 %copy.22 = f32[2,16,4,16,128]{4,3,2,1,0:T(8,128)} copy(f32[2,16,4,16,128]{4,3,2,1,0:T(8,128)} %bitcast.4) | data formatting | bytes 2097152
  82.2 0.0 copy-done
  82.2 0.7 copy.23
Async XLA Ops:
  79.8 2.4 %copy-start = (f32[256,256]{1,0:T(8,128)S(1)}, f32[256,256]{1,0:T(8,128)}, u32[]{:S(2)}) copy-start(f32[256,256]{1,0:T(8,128)} %get-tuple-element.5) | copy-start | bytes 786436

commit v2 on v1

v2 whole, which is shorter than its diff:
```python
import jax
import jax.numpy as jnp
from jax import lax
from jax.experimental import pallas as pl
from jax.experimental.pallas import tpu as pltpu
from jax.sharding import PartitionSpec as P

MESH = pl.DeviceIdType.MESH
bf16 = jnp.bfloat16
f32 = jnp.float32
i32 = jnp.int32

relaxation = 0.8
SPACE = 4
SHARD = 64
DEVS = SPACE * SHARD
ROWS = 4
KB = 16
KINDS_PAD = 384
CHUNKS = 2
PER = 16 // CHUNKS


def dot(a, b):
    return jnp.dot(a, b, preferred_element_type=f32)


def neighbours(v, x_low, x_high, y_low, y_high):
    y = lax.broadcasted_iota(i32, (4, 16, 128), 1)
    z = lax.broadcasted_iota(i32, (4, 16, 128), 2)
    v4 = v.reshape(4, 16, 128)
    total = jnp.concatenate([v4[1:], x_high[None]], axis=0) + jnp.concatenate([x_low[None], v4[:3]], axis=0)
    down = pltpu.roll(v, 1, 0).reshape(4, 16, 128)
    total = total + jnp.where(y == 0, y_low[:, None, :], down)
    up = pltpu.roll(v, 63, 0).reshape(4, 16, 128)
    total = total + jnp.where(y == 15, y_high[:, None, :], up)
    total = total + jnp.where(z == 0, 0.0, pltpu.roll(v, 1, 1).reshape(4, 16, 128))
    total = total + jnp.where(z == 127, 0.0, pltpu.roll(v, 127, 1).reshape(4, 16, 128))
    return total.reshape(64, 128)


def kernel(
    vf_hbm, src_hbm, material, mat_real, mat_loss, surface, near_boxes, nb_hbm, rad_hbm, interp_hbm,
    phase, far_parents, far_kind, tr_hbm,
    vol_hbm, forcing,
    v0, v1, v2, src, interp, rad, nblk, tr,
    diag, loss, rinv,
    sx, sy, hx, hy, hyf,
    a_sel, oh_sel, n3, pick,
    m2, m2t, cosines, sines,
    p_col, k_col, oh_far, tt, tt_t, tg,
    frows, pb, g, gg, i2f, i2b, r, left, force,
    in_sem, halo_send, halo_recv, t_send, t_recv, near_send, near_recv, a_send, a_recv, back_send, back_recv,
    self_sem, out_sem, line_sem, all_sem,
):
    space = lax.axis_index("space")
    shard = lax.axis_index("shard")
    me = space * SHARD + shard
    at_x, at_z, at_y = shard // 16, lax.rem(shard // 2, 8), lax.rem(shard, 2)
    my_kb = shard // 4
    my_j = lax.rem(shard, 4)
    my_e = space * 4 + my_j
    hop = shard + 2 * at_y - 1
    has_hop = jnp.logical_and(hop >= 0, hop < SHARD)

    def signal(sem, to):
        pl.semaphore_signal(sem, inc=1, device_id=to, device_id_type=MESH)

    x_line = [(space, lax.rem(at_x + k, 4) * 16 + at_z * 2 + at_y) for k in range(1, 4)]
    z_line = [(space, at_x * 16 + lax.rem(at_z + k, 8) * 2 + at_y) for k in range(1, 8)]
    y_group = [
        (lax.rem(space + s, 4), at_x * 16 + at_z * 2 + lax.rem(at_y + y, 2))
        for s in range(4)
        for y in range(2)
        if s or y
    ]
    barrier = pltpu.get_barrier_semaphore()
    for to in x_line + z_line + y_group + [(space, my_kb * 4 + 3 - my_j)]:
        signal(barrier, to)

    @pl.when(has_hop)
    def _():
        signal(barrier, (space, jnp.clip(hop, 0, SHARD - 1)))

    loads = [
        pltpu.make_async_copy(a, b, in_sem.at[n])
        for n, (a, b) in enumerate(
            [(vf_hbm, v0), (rad_hbm, rad), (interp_hbm, interp), (src_hbm, src), (tr_hbm, tr), (nb_hbm, nblk)]
        )
    ]
    for c in loads:
        c.start()

    mat = material[...].reshape(64, 128)
    d = jnp.full((64, 128), 6.0, f32)
    l = jnp.zeros((64, 128), f32)
    for m in range(8):
        here = mat == m
        d = d + jnp.where(here, mat_real[m], 0.0)
        l = l + jnp.where(here, mat_loss[m], 0.0)
    diag[...] = d
    loss[...] = l
    rinv[...] = relaxation / d

    @pl.when(space == 0)
    def _():
        hx[:, 0] = jnp.zeros((2, CHUNKS, 32 * PER, 128), bf16)

    @pl.when(space == SPACE - 1)
    def _():
        hx[:, 1] = jnp.zeros((2, CHUNKS, 32 * PER, 128), bf16)

    @pl.when(shard == 0)
    def _():
        hy[:, 0] = jnp.zeros((2, CHUNKS, 8 * PER, 128), bf16)
        n3[0:16] = jnp.zeros((16, 16, 256), bf16)

    @pl.when(shard == SHARD - 1)
    def _():
        hy[:, 1] = jnp.zeros((2, CHUNKS, 8 * PER, 128), bf16)
        n3[32:48] = jnp.zeros((16, 16, 256), bf16)

    loads[0].wait()

    def faces_y(w, ch, field):
        for side, y in ((0, 0), (1, 15)):
            for t in range(2):
                rows = field[pl.ds(t * 1024 + ch * PER * 64 + y, 4 * PER, stride=16), :]
                sy[w, side, ch, 4 * PER * t : 4 * PER * t + 4 * PER, :] = rows.astype(bf16)

    for ch in range(CHUNKS):
        for el in range(PER):
            for t in range(2):
                first = (t * 16 + ch * PER + el) * 64
                to = (el * 2 + t) * 16
                sx[0, 0, ch, to : to + 16, :] = v0[first : first + 16, :].astype(bf16)
                sx[0, 1, ch, to : to + 16, :] = v0[first + 48 : first + 64, :].astype(bf16)
        faces_y(0, ch, v0)

    def copy_to(src_ref, dst_ref, send, recv, to):
        return pltpu.make_async_remote_copy(
            src_ref=src_ref, dst_ref=dst_ref, send_sem=send, recv_sem=recv, device_id=to, device_id_type=MESH
        )

    low_x, high_x = (jnp.maximum(space - 1, 0), shard), (jnp.minimum(space + 1, SPACE - 1), shard)
    low_y, high_y = (space, jnp.maximum(shard - 1, 0)), (space, jnp.minimum(shard + 1, SHARD - 1))
    has = (space > 0, space < SPACE - 1, shard > 0, shard < SHARD - 1)

    def halo_copies(w, ch):
        return [
            copy_to(sx.at[w, 0, ch], hx.at[w, 1, ch], halo_send.at[w, ch, 0], halo_recv.at[w, ch, 1], low_x),
            copy_to(sx.at[w, 1, ch], hx.at[w, 0, ch], halo_send.at[w, ch, 1], halo_recv.at[w, ch, 0], high_x),
            copy_to(sy.at[w, 0, ch], hy.at[w, 1, ch], halo_send.at[w, ch, 2], halo_recv.at[w, ch, 3], low_y),
            copy_to(sy.at[w, 1, ch], hy.at[w, 0, ch], halo_send.at[w, ch, 3], halo_recv.at[w, ch, 2], high_y),
        ]

    def start_halo(w, ch):
        for sent, c in zip(has, halo_copies(w, ch)):
            pl.when(sent)(c.start)

    def wait_halo(w, ch):
        for k, c in enumerate(halo_copies(w, ch)):
            pl.when(has[k ^ 1])(c.wait_recv)
            pl.when(has[k])(c.wait_send)

    pl.semaphore_wait(barrier, 18 + has_hop.astype(i32))
    for ch in range(CHUNKS):
        start_halo(0, ch)
    for to in x_line:
        signal(line_sem, to)

    loads[1].wait()
    loads[2].wait()
    rad2 = rad[...].reshape(256, 512)

    def compose(kb, carry):
        cols = pl.multiple_of(kb * 128, 128)
        m = dot(rad2, interp[:, pl.ds(cols, 128)])
        m_re, m_im = m[:128], m[128:]
        both = jnp.concatenate(
            [jnp.concatenate([m_re, m_im], axis=1), jnp.concatenate([-m_im, m_re], axis=1)], axis=0
        )
        m2[kb] = both.astype(bf16)
        m2t[kb] = both.T.astype(bf16)
        angle = phase[:, pl.ds(cols, 128)]
        cosines[kb] = jnp.cos(angle)
        sines[kb] = jnp.sin(angle)
        return carry

    lax.fori_loop(0, KB // 2, compose, 0)
    pl.semaphore_wait(line_sem, 3)
    for to in z_line:
        signal(all_sem, to)

    def sweep(w, ch, old, new):
        for side in range(2):
            hyf[side] = hy[w, side, ch].astype(f32)

        def one(el, carry):
            e = ch * PER + el
            parts = []
            for t in range(2):
                te = t * 16 + e
                rows = pl.ds(pl.multiple_of(te * 64, 64), 64)
                v = old[rows, :]
                xr = pl.ds(pl.multiple_of((el * 2 + t) * 16, 16), 16)
                yr = pl.ds(pl.multiple_of((t * PER + el) * 4, 4), 4)
                near = neighbours(
                    v, hx[w, 0, ch, xr, :].astype(f32), hx[w, 1, ch, xr, :].astype(f32), hyf[0, yr, :], hyf[1, yr, :]
                )
                parts.append((te, rows, xr, v, near))
            dd, ll, rr = diag[...], loss[...], rinv[...]
            re, im = parts[0][3], parts[1][3]
            out_re = re + rr * (src[parts[0][1], :] - (dd * re - parts[0][4] - ll * im))
            out_im = im + rr * (src[parts[1][1], :] - (dd * im - parts[1][4] + ll * re))
            for (te, rows, xr, _, _), out in zip(parts, (out_re, out_im)):
                new[rows, :] = out
                narrow = out.astype(bf16)
                if w == 0:
                    sx[1, 0, ch, xr, :] = narrow[0:16]
                    sx[1, 1, ch, xr, :] = narrow[48:64]
                else:
                    ar = pl.ds(pl.multiple_of(te * 16, 16), 16)
                    for x in range(4):
                        a_sel[ar, 128 * x : 128 * x + 128] = narrow[16 * x : 16 * x + 16]
            return carry

        lax.fori_loop(0, PER, one, 0, unroll=2)

    loads[3].wait()
    for ch in range(CHUNKS):
        wait_halo(0, ch)
        sweep(0, ch, v0, v1)
        faces_y(1, ch, v1)
        start_halo(1, ch)
    lax.fori_loop(KB // 2, KB, compose, 0)

    def select_hot(i, carry):
        for h in range(2):
            cells = surface[pl.ds(2 * i + h, 1), :]
            want = (cells // 2048) * 128 + lax.rem(cells, 128)
            rows = lax.broadcasted_iota(i32, (512, 128), 0)
            oh_sel[i, :, 128 * h : 128 * h + 128] = jnp.where(rows == want, 1.0, 0.0).astype(bf16)
        return carry

    lax.fori_loop(0, 8, select_hot, 0)
    p_col[...] = far_parents[...].T
    k_col[...] = far_kind[...].T

    def far_hot(rb, carry):
        cols = p_col[pl.ds(pl.multiple_of(rb * 64, 64), 64), :]
        lanes = lax.broadcasted_iota(i32, (64, 512), 1)
        for f in range(8):
            oh_far[rb, 64 * f : 64 * f + 64, :] = jnp.where(cols[:, f : f + 1] == lanes, 1.0, 0.0).astype(bf16)
        return carry

    lax.fori_loop(0, 8, far_hot, 0)

    for ch in range(CHUNKS):
        wait_halo(1, ch)
        sweep(1, ch, v1, v2)
    out_copy = pltpu.make_async_copy(v2, vol_hbm, out_sem.at[0])
    out_copy.start()

    def pick_box(i, carry):
        got = dot(a_sel[...], oh_sel[i])
        pair = surface[pl.ds(2 * i, 2), :]
        for h in range(2):
            y = lax.rem(pair[h : h + 1] // 128, 16)
            keep = lax.broadcasted_iota(i32, (16, 128), 0) == y
            mine = got[:, 128 * h : 128 * h + 128].reshape(32, 16, 128)
            mine = jnp.sum(jnp.where(keep[None], mine, 0.0), axis=1).astype(bf16)
            n3[16 + 2 * i + h] = jnp.concatenate([mine[:16], mine[16:]], axis=1)
        return carry

    lax.fori_loop(0, 8, pick_box, 0, unroll=2)

    cur = n3[16:32].reshape(256, 256)

    def near_copies():
        mid = n3.at[pl.ds(16, 16)]
        return [
            (has[2], copy_to(mid, n3.at[pl.ds(32, 16)], near_send.at[0], near_recv.at[0], low_y)),
            (has[3], copy_to(mid, n3.at[pl.ds(0, 16)], near_send.at[1], near_recv.at[1], high_y)),
        ]

    def pattern(i):
        kb = lax.rem(my_kb + 1 + i, KB)
        spread = dot(cur, m2[kb])
        for p in range(2):
            re = jnp.zeros((16, 128), f32)
            im = jnp.zeros((16, 128), f32)
            for c in range(8):
                rows = spread[(p * 8 + c) * 16 : (p * 8 + c) * 16 + 16]
                s_re, s_im = rows[:, :128], rows[:, 128:]
                co, si = cosines[kb, c : c + 1, :], sines[kb, c : c + 1, :]
                re = re + (co * s_re - si * s_im)
                im = im + (si * s_re + co * s_im)
            frows[pl.ds(2 * p, 16, stride=4), :] = re
            frows[pl.ds(2 * p + 1, 16, stride=4), :] = im
        pb[pl.ds(pl.multiple_of(kb * 64, 64), 64), :] = frows[...].astype(bf16)

    my_rows = pl.ds(pl.multiple_of(me * ROWS, ROWS), ROWS)
    my_slot = pl.ds(pl.multiple_of((my_kb * 16 + my_e) * ROWS, ROWS), ROWS)
    owners = [lax.rem(my_e + j, 16) for j in range(16)]
    owner_space = [e // 4 for e in owners]
    owner_j = [lax.rem(e, 4) for e in owners]

    def send_pattern(i, first):
        kb = lax.rem(my_kb + 1 + i, KB)
        for j in range(first, 16):
            from_rows = pl.ds(pl.multiple_of(kb * 64 + owners[j] * ROWS, ROWS), ROWS)
            copy_to(
                pb.at[from_rows], g.at[my_rows], a_send.at[0], a_recv.at[0], (owner_space[j], kb * 4 + owner_j[j])
            ).start()

    pattern(0)
    for sent, c in near_copies():
        pl.when(sent)(c.start)
    pl.semaphore_wait(all_sem, 7)

    def step_out(i, carry):
        send_pattern(i - 1, 0)
        pattern(i)
        return carry

    lax.fori_loop(1, KB, step_out, 0)

    def t_copy(step):
        rows = pl.ds(pl.multiple_of(my_j * 32, 32), 32)
        to = (space, my_kb * 4 + lax.rem(my_j + step, 4))
        return copy_to(tt.at[:, rows, :], tt.at[:, rows, :], t_send.at[step - 1], t_recv.at[step - 1], to)

    loads[4].wait()
    t_rows = pl.ds(pl.multiple_of(my_j * 32, 32), 32)
    for c in range(2):
        tt[c, t_rows, 256:KINDS_PAD] = jnp.zeros((32, KINDS_PAD - 256), bf16)
        tt[c, t_rows, 0:316] = tr[c].astype(bf16)

    send_pattern(KB - 1, 1)
    own = pltpu.make_async_copy(pb.at[my_slot], g.at[my_rows], self_sem.at[0])
    own.start()
    for step in (1, 2, 3):
        t_copy(step).start()

    sides = near_copies()
    pl.when(has[3])(sides[0][1].wait_recv)
    pl.when(has[2])(sides[1][1].wait_recv)
    for sent, c in sides:
        pl.when(sent)(c.wait_send)
    base = me * 16 - 16
    for s in range(4):
        for b in range(16):
            pick[16 * b : 16 * b + 16, 256 * s : 256 * s + 256] = n3[jnp.clip(near_boxes[s, b] - base, 0, 47)]
    loads[5].wait()
    force[...] = dot(pick[...], nblk[...].reshape(1024, 256))

    for step in (1, 2, 3):
        t_copy(step).wait_recv()
        t_copy(step).wait_send()
    for c in range(2):
        tt_t[:, 128 * c : 128 * c + 128] = tt[c].astype(f32).T.astype(bf16)

    def operators(rb, carry):
        cols = k_col[pl.ds(pl.multiple_of(rb * 64, 64), 64), :]
        kinds = lax.broadcasted_iota(i32, (64, KINDS_PAD), 1)
        hot = [jnp.where(cols[:, f : f + 1] == kinds, 1.0, 0.0).astype(bf16) for f in range(8)]
        tg[rb] = dot(jnp.concatenate(hot, axis=0), tt_t[...])
        return carry

    lax.fori_loop(0, 8, operators, 0)

    own.wait()
    count = pl.ds(0, (DEVS - 1) * ROWS)
    arrived = copy_to(pb.at[count], g.at[count], a_send.at[0], a_recv.at[0], (space, shard))
    arrived.wait_recv()

    gg[:, 0:128] = g[pl.ds(0, 512, stride=2), :]
    gg[:, 128:256] = g[pl.ds(1, 512, stride=2), :]
    my_low = lax.rem(me, 32)

    def far(i):
        rb = lax.rem(me // 32 + 1 + i, 8)
        got = dot(oh_far[rb], gg[...])
        t = tg[rb]
        re = jnp.zeros((64, 128), f32)
        im = jnp.zeros((64, 128), f32)
        for f in range(8):
            at = slice(64 * f, 64 * f + 64)
            g_re, g_im, t_re, t_im = got[at, :128], got[at, 128:], t[at, :128], t[at, 128:]
            re = re + (t_re * g_re - t_im * g_im)
            im = im + (t_im * g_re + t_re * g_im)
        i2f[pl.ds(0, 64, stride=2), :] = re
        i2f[pl.ds(1, 64, stride=2), :] = im
        i2b[pl.ds(pl.multiple_of(rb * 128, 128), 128), :] = i2f[...].astype(bf16)

    def send_back(i, first):
        rb = lax.rem(me // 32 + 1 + i, 8)
        for j in range(first, 32):
            low = lax.rem(my_low + j, 32)
            rows = pl.ds(pl.multiple_of((rb * 32 + low) * ROWS, ROWS), ROWS)
            to = (rb // 2, lax.rem(rb, 2) * 32 + low)
            copy_to(i2b.at[rows], r.at[my_slot], back_send.at[0], back_recv.at[my_kb], to).start()

    far(0)

    def step_back(i, carry):
        send_back(i - 1, 0)
        far(i)
        return carry

    lax.fori_loop(1, 8, step_back, 0)
    arrived.wait_send()
    send_back(7, 1)
    own_back = pltpu.make_async_copy(i2b.at[my_rows], r.at[my_slot], self_sem.at[1])
    own_back.start()
    own_back.wait()
    out_copy.wait()

    def bring(i, carry):
        kb = lax.rem(my_kb + i, KB)

        def wait_rows(n):
            rows = pl.ds(0, n)
            copy_to(i2b.at[rows], r.at[rows], back_send.at[0], back_recv.at[kb], (space, shard)).wait_recv()

        pl.when(i == 0)(lambda: wait_rows(60))
        pl.when(i > 0)(lambda: wait_rows(64))
        frows[...] = r[pl.ds(pl.multiple_of(kb * 64, 64), 64), :].astype(f32)
        for p in range(2):
            x_re = frows[pl.ds(2 * p, 16, stride=4), :]
            x_im = frows[pl.ds(2 * p + 1, 16, stride=4), :]
            for c in range(8):
                co, si = cosines[kb, c : c + 1, :], sines[kb, c : c + 1, :]
                at = (p * 8 + c) * 16
                left[at : at + 16, 0:128] = (co * x_re + si * x_im).astype(bf16)
                left[at : at + 16, 128:256] = (co * x_im - si * x_re).astype(bf16)
        force[...] += dot(left[...], m2t[kb])
        return carry

    lax.fori_loop(0, KB, bring, 0)
    copy_to(i2b.at[count], r.at[count], back_send.at[0], back_recv.at[0], (space, shard)).wait_send()
    forcing[...] = force[...]


def shards(
    volume_field, source, material, mat_real, mat_loss, surface_map, near_boxes, near_blocks, radiate, interp,
    phase_angle, far_parents, far_kind, translate,
):
    shape = volume_field.shape
    any_ = pl.BlockSpec(memory_space=pl.ANY)
    vmem = pl.BlockSpec(memory_space=pltpu.VMEM)
    smem = pl.BlockSpec(memory_space=pltpu.SMEM)
    V = pltpu.VMEM
    dma = pltpu.SemaphoreType.DMA
    volume, forcing = pl.pallas_call(
        kernel,
        out_shape=(jax.ShapeDtypeStruct((2048, 128), f32), jax.ShapeDtypeStruct((256, 256), f32)),
        in_specs=[any_, any_, vmem, smem, smem, vmem, smem, any_, any_, any_, vmem, vmem, vmem, any_],
        out_specs=(any_, vmem),
        scratch_shapes=[
            V((2048, 128), f32), V((2048, 128), f32), V((2048, 128), f32), V((2048, 128), f32),
            V((512, 2048), bf16), V((2, 128, 512), bf16), V((4, 256, 256), bf16), V((2, 32, 316), f32),
            V((64, 128), f32), V((64, 128), f32), V((64, 128), f32),
            V((2, 2, CHUNKS, 32 * PER, 128), bf16), V((2, 2, CHUNKS, 8 * PER, 128), bf16),
            V((2, 2, CHUNKS, 32 * PER, 128), bf16), V((2, 2, CHUNKS, 8 * PER, 128), bf16), V((2, 8 * PER, 128), f32),
            V((512, 512), bf16), V((8, 512, 256), bf16), V((48, 16, 256), bf16), V((256, 1024), bf16),
            V((16, 256, 256), bf16), V((16, 256, 256), bf16), V((16, 8, 128), f32), V((16, 8, 128), f32),
            V((512, 8), i32), V((512, 8), i32), V((8, 512, 512), bf16),
            V((2, 128, KINDS_PAD), bf16), V((KINDS_PAD, 256), bf16), V((8, 512, 256), f32),
            V((64, 128), f32), V((1024, 128), bf16), V((1024, 128), bf16), V((512, 256), bf16),
            V((128, 128), f32), V((1024, 128), bf16), V((1024, 128), bf16), V((256, 256), bf16), V((256, 256), f32),
            dma((6,)), dma((2, CHUNKS, 4)), dma((2, CHUNKS, 4)), dma((3,)), dma((3,)), dma((2,)), dma((2,)),
            dma((1,)), dma((1,)), dma((1,)), dma((KB,)), dma((2,)), dma((1,)),
            pltpu.SemaphoreType.REGULAR, pltpu.SemaphoreType.REGULAR,
        ],
        compiler_params=pltpu.CompilerParams(collective_id=3, has_side_effects=True),
        name="relax_and_couple",
    )(
        volume_field.reshape(2048, 128), source.reshape(2048, 128), material, mat_real, mat_loss, surface_map,
        near_boxes.T, near_blocks, radiate, interp, phase_angle, far_parents.T, far_kind.T, translate.transpose(1, 2, 0),
    )
    return volume.reshape(shape), forcing.reshape(16, 16, 256)


def solution(mesh):
    return jax.shard_map(
        shards,
        mesh=mesh,
        in_specs=(
            P(None, None, "space", "shard", None),
            P(None, None, "space", "shard", None),
            P("space", "shard", None),
            P(),
            P(),
            P(("space", "shard"), None),
            P(("space", "shard"), None),
            P(),
            P(),
            P(),
            P(),
            P(),
            P(),
            P(None, None, "shard"),
        ),
        out_specs=(P(None, None, "space", "shard", None), P(("space", "shard"), None, None)),
        check_vma=False,
    )
```

time: 83.2 us -> 57.3 us (0.69)
  Pallas kernels: 72.9 us -> 53.5 us
  local copies, waits for them, and re-layouts: 9.32 us -> 3.06 us
    pallas_call x1, Pallas kernels: 72.9 us -> 53.5 us  [shards(): pl.pallas_call(kernel, out_shape=(jax.ShapeDtypeStruct((2048, 128), f32),...]
    unnamed x8 -> x4, local copies, waits for them, and re-layouts: 9.32 us -> 3.06 us
where the time goes in v2:
time: 57.3 us; the launch traced here: 57.2 us
  Pallas kernels  53.5 us (93%)
  local copies, waits for them, and re-layouts  3.06 us (5%)
  between operations  0.65 us (1%)
    pallas_call x1, Pallas kernels, shards(): pl.pallas_call(kernel, out_shape=(jax.ShapeDtypeStruct((2048, 128), f32),...  53.5 us
    unnamed x4, local copies, waits for them, and re-layouts  3.06 us

profile of v2, /device:TPU:1, one launch (start us, length us, event | category | flops | bytes accessed | tf_op | source)
XLA Modules:
  0.0 57.2 jit_solution(2552175515610904466)
XLA Ops:
  0.6 53.5 %relax_and_couple.1 = (f32[2048,128]{1,0:T(8,128)}, f32[256,256]{1,0:T(8,128)}) custom-call(f32[2048,128]{1,0:T(8,128)} %bitcast.9, f32[2048,128]{1,0:T(8,128)} %bitcast.10, s32[4,16,128]{2,1,0:T(8,128)} %material.1, f32[8]{0:T(128)} %mat_real.1, f32[8]{0:T(128)} %mat_loss.1, s32[16,128]{1,0:T(8,128)} %surface.1, s32[4,16]{1,0:T(4,128)} %bitcast.15, ...), custom_call_target="tpu_custom_call" | custom-call | tf_op jit(solution)/shard_map/relax_and_couple/pallas_call | solution.py:456
  54.1 0.0 copy-start
  54.1 2.4 %copy.18 = f32[2,16,4,16,128]{4,3,2,1,0:T(8,128)} copy(f32[2,16,4,16,128]{4,3,2,1,0:T(8,128)} %bitcast.8) | data formatting | bytes 2097152
  56.5 0.0 copy-done
  56.5 0.7 %copy.19 = f32[16,16,256]{2,1,0:T(8,128)} copy(f32[16,16,256]{2,1,0:T(8,128)S(1)} %bitcast.11) | data formatting | bytes 524288
Async XLA Ops:
  54.1 2.4 %copy-start = (f32[256,256]{1,0:T(8,128)S(1)}, f32[256,256]{1,0:T(8,128)}, u32[]{:S(2)}) copy-start(f32[256,256]{1,0:T(8,128)} %get-tuple-element.5) | copy-start | bytes 786436

commit v3 on v2

--- a/solution.py
+++ b/solution.py
@@ -62,6 +62,21 @@
     my_e = space * 4 + my_j
     hop = shard + 2 * at_y - 1
     has_hop = jnp.logical_and(hop >= 0, hop < SHARD)
+
+    def turn(start, by, period):
+        at = start + by
+        return jnp.where(at >= period, at - period, at)
+
+    def quarter(n):
+        return pl.ds(pl.multiple_of(n * ROWS, ROWS), ROWS)
+
+    def far_first(m):
+        return jnp.where(m == 0, 2, jnp.where(m == 1, 1, jnp.where(m == 2, 3, 0)))
+
+    my_zh = lax.rem(my_kb, 4)
+
+    def block_at(i):
+        return turn(at_x, far_first(lax.rem(i, 4)), 4) * 4 + turn(my_zh, far_first(i // 4), 4)
 
     def signal(sem, to):
         pl.semaphore_signal(sem, inc=1, device_id=to, device_id_type=MESH)
@@ -247,17 +262,22 @@
     p_col[...] = far_parents[...].T
     k_col[...] = far_kind[...].T
 
-    def far_hot(rb, carry):
-        cols = p_col[pl.ds(pl.multiple_of(rb * 64, 64), 64), :]
-        lanes = lax.broadcasted_iota(i32, (64, 512), 1)
-        for f in range(8):
-            oh_far[rb, 64 * f : 64 * f + 64, :] = jnp.where(cols[:, f : f + 1] == lanes, 1.0, 0.0).astype(bf16)
-        return carry
-
-    lax.fori_loop(0, 8, far_hot, 0)
+    def t_copy(step):
+        rows = pl.ds(pl.multiple_of(my_j * 32, 32), 32)
+        to = (space, my_kb * 4 + lax.rem(my_j + step, 4))
+        return copy_to(tt.at[:, rows, :], tt.at[:, rows, :], t_send.at[step - 1], t_recv.at[step - 1], to)
+
+    loads[4].wait()
+    t_rows = pl.ds(pl.multiple_of(my_j * 32, 32), 32)
+    for c in range(2):
+        tt[c, t_rows, 256:KINDS_PAD] = jnp.zeros((32, KINDS_PAD - 256), bf16)
+        tt[c, t_rows, 0:316] = tr[c].astype(bf16)
 
     for ch in range(CHUNKS):
         wait_halo(1, ch)
+        if ch == CHUNKS - 1:
+            for step in (1, 2, 3):
+                t_copy(step).start()
         sweep(1, ch, v1, v2)
     out_copy = pltpu.make_async_copy(v2, vol_hbm, out_sem.at[0])
     out_copy.start()
@@ -285,7 +305,7 @@
         ]
 
     def pattern(i):
-        kb = lax.rem(my_kb + 1 + i, KB)
+        kb = block_at(i)
         spread = dot(cur, m2[kb])
         for p in range(2):
             re = jnp.zeros((16, 128), f32)
@@ -298,50 +318,117 @@
                 im = im + (si * s_re + co * s_im)
             frows[pl.ds(2 * p, 16, stride=4), :] = re
             frows[pl.ds(2 * p + 1, 16, stride=4), :] = im
-        pb[pl.ds(pl.multiple_of(kb * 64, 64), 64), :] = frows[...].astype(bf16)
+        pb[pl.ds(kb * 4, 4)] = frows[...].astype(bf16).reshape(4, 16, 128)
 
     my_rows = pl.ds(pl.multiple_of(me * ROWS, ROWS), ROWS)
     my_slot = pl.ds(pl.multiple_of((my_kb * 16 + my_e) * ROWS, ROWS), ROWS)
-    owners = [lax.rem(my_e + j, 16) for j in range(16)]
-    owner_space = [e // 4 for e in owners]
-    owner_j = [lax.rem(e, 4) for e in owners]
-
-    def send_pattern(i, first):
-        kb = lax.rem(my_kb + 1 + i, KB)
-        for j in range(first, 16):
-            from_rows = pl.ds(pl.multiple_of(kb * 64 + owners[j] * ROWS, ROWS), ROWS)
+
+    to_space = [turn(space, k, SPACE) for k in (2, 3, 1, 0)]
+    to_j = [turn(my_j, k, 4) for k in (3, 2, 1, 0)]
+
+    def send_pattern(i, count):
+        kb = block_at(i)
+        for n in range(count):
+            q, j = to_space[n // 4], to_j[n % 4]
             copy_to(
-                pb.at[from_rows], g.at[my_rows], a_send.at[0], a_recv.at[0], (owner_space[j], kb * 4 + owner_j[j])
+                pb.at[kb * 4 + q, quarter(j)], g.at[my_rows], a_send.at[0], a_recv.at[0], (q, kb * 4 + j)
             ).start()
 
     pattern(0)
+    pl.semaphore_wait(all_sem, 7)
+
+    def step_out(i, carry):
+        send_pattern(i - 1, 16)
+        pattern(i)
+        return carry
+
+    lax.fori_loop(1, KB, step_out, 0)
+
+    send_pattern(KB - 1, 15)
+    own = pltpu.make_async_copy(pb.at[my_kb * 4 + space, quarter(my_j)], g.at[my_rows], self_sem.at[0])
+    own.start()
+
     for sent, c in near_copies():
         pl.when(sent)(c.start)
-    pl.semaphore_wait(all_sem, 7)
-
-    def step_out(i, carry):
-        send_pattern(i - 1, 0)
-        pattern(i)
-        return carry
-
-    lax.fori_loop(1, KB, step_out, 0)
-
-    def t_copy(step):
-        rows = pl.ds(pl.multiple_of(my_j * 32, 32), 32)
-        to = (space, my_kb * 4 + lax.rem(my_j + step, 4))
-        return copy_to(tt.at[:, rows, :], tt.at[:, rows, :], t_send.at[step - 1], t_recv.at[step - 1], to)
-
-    loads[4].wait()
-    t_rows = pl.ds(pl.multiple_of(my_j * 32, 32), 32)
+    def block_rows(col, rb):
+        first = (rb // 4) * 64 + lax.rem(rb, 4) * 8
+        at = [first + q * 128 + x * 32 for q in range(SPACE) for x in range(2)]
+        return jnp.concatenate([col[pl.ds(pl.multiple_of(n, 8), 8), :] for n in at], axis=0)
+
+    def far_hot(rb, carry):
+        cols = block_rows(p_col, rb)
+        lanes = lax.broadcasted_iota(i32, (64, 512), 1)
+        for f in range(8):
+            oh_far[rb, 64 * f : 64 * f + 64, :] = jnp.where(cols[:, f : f + 1] == lanes, 1.0, 0.0).astype(bf16)
+        return carry
+
+    lax.fori_loop(0, 8, far_hot, 0)
+
+    for step in (1, 2, 3):
+        t_copy(step).wait_recv()
+        t_copy(step).wait_send()
     for c in range(2):
-        tt[c, t_rows, 256:KINDS_PAD] = jnp.zeros((32, KINDS_PAD - 256), bf16)
-        tt[c, t_rows, 0:316] = tr[c].astype(bf16)
-
-    send_pattern(KB - 1, 1)
-    own = pltpu.make_async_copy(pb.at[my_slot], g.at[my_rows], self_sem.at[0])
-    own.start()
-    for step in (1, 2, 3):
-        t_copy(step).start()
+        tt_t[:, 128 * c : 128 * c + 128] = tt[c].astype(f32).T.astype(bf16)
+
+    def operators(rb, carry):
+        cols = block_rows(k_col, rb)
+        kinds = lax.broadcasted_iota(i32, (64, KINDS_PAD), 1)
+        hot = [jnp.where(cols[:, f : f + 1] == kinds, 1.0, 0.0).astype(bf16) for f in range(8)]
+        tg[rb] = dot(jnp.concatenate(hot, axis=0), tt_t[...])
+        return carry
+
+    lax.fori_loop(0, 8, operators, 0)
+
+    own.wait()
+    count = pl.ds(0, (DEVS - 1) * ROWS)
+    arrived = copy_to(g.at[count], g.at[count], a_send.at[0], a_recv.at[0], (space, shard))
+    arrived.wait_recv()
+
+    gg[:, 0:128] = g[pl.ds(0, 512, stride=2), :]
+    gg[:, 128:256] = g[pl.ds(1, 512, stride=2), :]
+    my_xh, my_xl = at_x // 2, lax.rem(at_x, 2)
+    to_xl = [1 - my_xl, my_xl]
+
+    def target_block(i):
+        return turn(my_xh, 1 - lax.rem(i, 2), 2) * 4 + turn(my_zh, far_first(i // 2), 4)
+
+    def far(i):
+        rb = target_block(i)
+        got = dot(oh_far[rb], gg[...])
+        t = tg[rb]
+        re = jnp.zeros((64, 128), f32)
+        im = jnp.zeros((64, 128), f32)
+        for f in range(8):
+            at = slice(64 * f, 64 * f + 64)
+            g_re, g_im, t_re, t_im = got[at, :128], got[at, 128:], t[at, :128], t[at, 128:]
+            re = re + (t_re * g_re - t_im * g_im)
+            im = im + (t_im * g_re + t_re * g_im)
+        i2f[pl.ds(0, 64, stride=2), :] = re
+        i2f[pl.ds(1, 64, stride=2), :] = im
+        i2b[pl.ds(rb * 8, 8)] = i2f[...].astype(bf16).reshape(8, 16, 128)
+
+    def send_back(i, count):
+        rb = target_block(i)
+        first = (rb // 4) * 32 + lax.rem(rb, 4) * 4
+        for n in range(count):
+            q, x, j = to_space[n // 8], to_xl[n // 4 % 2], to_j[n % 4]
+            copy_to(
+                i2b.at[rb * 8 + q * 2 + x, quarter(j)], r.at[my_slot], back_send.at[0], back_recv.at[my_kb],
+                (q, first + x * 16 + j),
+            ).start()
+
+    far(0)
+
+    def step_back(i, carry):
+        send_back(i - 1, 32)
+        far(i)
+        return carry
+
+    lax.fori_loop(1, 8, step_back, 0)
+    arrived.wait_send()
+    send_back(7, 31)
+    own_back = pltpu.make_async_copy(i2b.at[(my_xh * 4 + my_zh) * 8 + space * 2 + my_xl, quarter(my_j)], r.at[my_slot], self_sem.at[1])
+    own_back.start()
 
     sides = near_copies()
     pl.when(has[3])(sides[0][1].wait_recv)
@@ -355,77 +442,18 @@
     loads[5].wait()
     force[...] = dot(pick[...], nblk[...].reshape(1024, 256))
 
-    for step in (1, 2, 3):
-        t_copy(step).wait_recv()
-        t_copy(step).wait_send()
-    for c in range(2):
-        tt_t[:, 128 * c : 128 * c + 128] = tt[c].astype(f32).T.astype(bf16)
-
-    def operators(rb, carry):
-        cols = k_col[pl.ds(pl.multiple_of(rb * 64, 64), 64), :]
-        kinds = lax.broadcasted_iota(i32, (64, KINDS_PAD), 1)
-        hot = [jnp.where(cols[:, f : f + 1] == kinds, 1.0, 0.0).astype(bf16) for f in range(8)]
-        tg[rb] = dot(jnp.concatenate(hot, axis=0), tt_t[...])
-        return carry
-
-    lax.fori_loop(0, 8, operators, 0)
-
-    own.wait()
-    count = pl.ds(0, (DEVS - 1) * ROWS)
-    arrived = copy_to(pb.at[count], g.at[count], a_send.at[0], a_recv.at[0], (space, shard))
-    arrived.wait_recv()
-
-    gg[:, 0:128] = g[pl.ds(0, 512, stride=2), :]
-    gg[:, 128:256] = g[pl.ds(1, 512, stride=2), :]
-    my_low = lax.rem(me, 32)
-
-    def far(i):
-        rb = lax.rem(me // 32 + 1 + i, 8)
-        got = dot(oh_far[rb], gg[...])
-        t = tg[rb]
-        re = jnp.zeros((64, 128), f32)
-        im = jnp.zeros((64, 128), f32)
-        for f in range(8):
-            at = slice(64 * f, 64 * f + 64)
-            g_re, g_im, t_re, t_im = got[at, :128], got[at, 128:], t[at, :128], t[at, 128:]
-            re = re + (t_re * g_re - t_im * g_im)
-            im = im + (t_im * g_re + t_re * g_im)
-        i2f[pl.ds(0, 64, stride=2), :] = re
-        i2f[pl.ds(1, 64, stride=2), :] = im
-        i2b[pl.ds(pl.multiple_of(rb * 128, 128), 128), :] = i2f[...].astype(bf16)
-
-    def send_back(i, first):
-        rb = lax.rem(me // 32 + 1 + i, 8)
-        for j in range(first, 32):
-            low = lax.rem(my_low + j, 32)
-            rows = pl.ds(pl.multiple_of((rb * 32 + low) * ROWS, ROWS), ROWS)
-            to = (rb // 2, lax.rem(rb, 2) * 32 + low)
-            copy_to(i2b.at[rows], r.at[my_slot], back_send.at[0], back_recv.at[my_kb], to).start()
-
-    far(0)
-
-    def step_back(i, carry):
-        send_back(i - 1, 0)
-        far(i)
-        return carry
-
-    lax.fori_loop(1, 8, step_back, 0)
-    arrived.wait_send()
-    send_back(7, 1)
-    own_back = pltpu.make_async_copy(i2b.at[my_rows], r.at[my_slot], self_sem.at[1])
-    own_back.start()
     own_back.wait()
     out_copy.wait()
 
     def bring(i, carry):
-        kb = lax.rem(my_kb + i, KB)
+        kb = block_at(i)
 
         def wait_rows(n):
             rows = pl.ds(0, n)
-            copy_to(i2b.at[rows], r.at[rows], back_send.at[0], back_recv.at[kb], (space, shard)).wait_recv()
-
-        pl.when(i == 0)(lambda: wait_rows(60))
-        pl.when(i > 0)(lambda: wait_rows(64))
+            copy_to(r.at[rows], r.at[rows], back_send.at[0], back_recv.at[kb], (space, shard)).wait_recv()
+
+        pl.when(i == KB - 1)(lambda: wait_rows(60))
+        pl.when(i < KB - 1)(lambda: wait_rows(64))
         frows[...] = r[pl.ds(pl.multiple_of(kb * 64, 64), 64), :].astype(f32)
         for p in range(2):
             x_re = frows[pl.ds(2 * p, 16, stride=4), :]
@@ -439,7 +467,7 @@
         return carry
 
     lax.fori_loop(0, KB, bring, 0)
-    copy_to(i2b.at[count], r.at[count], back_send.at[0], back_recv.at[0], (space, shard)).wait_send()
+    copy_to(r.at[count], r.at[count], back_send.at[0], back_recv.at[0], (space, shard)).wait_send()
     forcing[...] = force[...]
 
 
@@ -468,8 +496,8 @@
             V((16, 256, 256), bf16), V((16, 256, 256), bf16), V((16, 8, 128), f32), V((16, 8, 128), f32),
             V((512, 8), i32), V((512, 8), i32), V((8, 512, 512), bf16),
             V((2, 128, KINDS_PAD), bf16), V((KINDS_PAD, 256), bf16), V((8, 512, 256), f32),
-            V((64, 128), f32), V((1024, 128), bf16), V((1024, 128), bf16), V((512, 256), bf16),
-            V((128, 128), f32), V((1024, 128), bf16), V((1024, 128), bf16), V((256, 256), bf16), V((256, 256), f32),
+            V((64, 128), f32), V((64, 16, 128), bf16), V((1024, 128), bf16), V((512, 256), bf16),
+            V((128, 128), f32), V((64, 16, 128), bf16), V((1024, 128), bf16), V((256, 256), bf16), V((256, 256), f32),
             dma((6,)), dma((2, CHUNKS, 4)), dma((2, CHUNKS, 4)), dma((3,)), dma((3,)), dma((2,)), dma((2,)),
             dma((1,)), dma((1,)), dma((1,)), dma((KB,)), dma((2,)), dma((1,)),
             pltpu.SemaphoreType.REGULAR, pltpu.SemaphoreType.REGULAR,

time: 57.3 us -> 52.3 us (0.913)
  Pallas kernels: 53.5 us -> 48.4 us
    pallas_call x1, Pallas kernels: 53.5 us -> 48.4 us  [shards(): pl.pallas_call(kernel, out_shape=(jax.ShapeDtypeStruct((2048, 128), f32),...]
where the time goes in v3:
time: 52.3 us; the launch traced here: 52.1 us
  Pallas kernels  48.4 us (93%)
  local copies, waits for them, and re-layouts  3.06 us (6%)
  between operations  0.65 us (1%)
    pallas_call x1, Pallas kernels, shards(): pl.pallas_call(kernel, out_shape=(jax.ShapeDtypeStruct((2048, 128), f32),...  48.4 us
    unnamed x4, local copies, waits for them, and re-layouts  3.06 us

profile of v3, /device:TPU:1, one launch (start us, length us, event | category | flops | bytes accessed | tf_op | source)
XLA Modules:
  0.0 52.1 jit_solution(16604639894456374145)
XLA Ops:
  0.6 48.4 %relax_and_couple.1 = (f32[2048,128]{1,0:T(8,128)}, f32[256,256]{1,0:T(8,128)}) custom-call(f32[2048,128]{1,0:T(8,128)} %bitcast.9, f32[2048,128]{1,0:T(8,128)} %bitcast.10, s32[4,16,128]{2,1,0:T(8,128)} %material.1, f32[8]{0:T(128)} %mat_real.1, f32[8]{0:T(128)} %mat_loss.1, s32[16,128]{1,0:T(8,128)} %surface.1, s32[4,16]{1,0:T(4,128)} %bitcast.15, ...), custom_call_target="tpu_custom_call" | custom-call | tf_op jit(solution)/shard_map/relax_and_couple/pallas_call | solution.py:484
  49.1 0.0 copy-start
  49.1 2.4 %copy.18 = f32[2,16,4,16,128]{4,3,2,1,0:T(8,128)} copy(f32[2,16,4,16,128]{4,3,2,1,0:T(8,128)} %bitcast.8) | data formatting | bytes 2097152
  51.4 0.0 copy-done
  51.4 0.7 %copy.19 = f32[16,16,256]{2,1,0:T(8,128)} copy(f32[16,16,256]{2,1,0:T(8,128)S(1)} %bitcast.11) | data formatting | bytes 524288
Async XLA Ops:
  49.1 2.4 %copy-start = (f32[256,256]{1,0:T(8,128)S(1)}, f32[256,256]{1,0:T(8,128)}, u32[]{:S(2)}) copy-start(f32[256,256]{1,0:T(8,128)} %get-tuple-element.5) | copy-start | bytes 786436

commit v4 on v3

--- a/solution.py
+++ b/solution.py
@@ -17,8 +17,9 @@
 ROWS = 4
 KB = 16
 KINDS_PAD = 384
-CHUNKS = 2
+CHUNKS = 4
 PER = 16 // CHUNKS
+VMEM_A = 58 * 1024 * 1024
 
 
 def dot(a, b):
@@ -40,10 +41,11 @@
 
 
 def kernel(
-    vf_hbm, src_hbm, material, mat_real, mat_loss, surface, near_boxes, nb_hbm, rad_hbm, interp_hbm,
-    phase, far_parents, far_kind, tr_hbm,
-    vol_hbm, forcing,
-    v0, v1, v2, src, interp, rad, nblk, tr,
+    vf_hbm, src_hbm, material_hbm, real_hbm, loss_hbm, surface_hbm, boxes_hbm, nb_hbm, rad_hbm, interp_hbm,
+    phase_hbm, parents_hbm, kind_hbm, tr_hbm,
+    v2, forcing,
+    v0, v1, src, interp, rad, nblk, tr,
+    material, mat_real, mat_loss, surface, near_boxes, phase, far_parents, far_kind,
     diag, loss, rinv,
     sx, sy, hx, hy, hyf,
     a_sel, oh_sel, n3, pick,
@@ -51,7 +53,7 @@
     p_col, k_col, oh_far, tt, tt_t, tg,
     frows, pb, g, gg, i2f, i2b, r, left, force,
     in_sem, halo_send, halo_recv, t_send, t_recv, near_send, near_recv, a_send, a_recv, back_send, back_recv,
-    self_sem, out_sem, line_sem, all_sem,
+    self_sem, line_sem, all_sem,
 ):
     space = lax.axis_index("space")
     shard = lax.axis_index("shard")
@@ -100,12 +102,18 @@
     loads = [
         pltpu.make_async_copy(a, b, in_sem.at[n])
         for n, (a, b) in enumerate(
-            [(vf_hbm, v0), (rad_hbm, rad), (interp_hbm, interp), (src_hbm, src), (tr_hbm, tr), (nb_hbm, nblk)]
+            [
+                (vf_hbm, v0), (rad_hbm, rad), (interp_hbm, interp), (src_hbm, src), (tr_hbm, tr), (nb_hbm, nblk),
+                (material_hbm, material), (real_hbm, mat_real), (loss_hbm, mat_loss), (phase_hbm, phase),
+                (surface_hbm, surface), (parents_hbm, far_parents), (kind_hbm, far_kind), (boxes_hbm, near_boxes),
+            ]
         )
     ]
-    for c in loads:
-        c.start()
-
+    for n in (6, 7, 8, 0, 3, 1, 2, 9, 4, 10, 11, 12, 13, 5):
+        loads[n].start()
+
+    for n in (6, 7, 8):
+        loads[n].wait()
     mat = material[...].reshape(64, 128)
     d = jnp.full((64, 128), 6.0, f32)
     l = jnp.zeros((64, 128), f32)
@@ -186,6 +194,7 @@
 
     loads[1].wait()
     loads[2].wait()
+    loads[9].wait()
     rad2 = rad[...].reshape(256, 512)
 
     def compose(kb, carry):
@@ -250,6 +259,8 @@
         start_halo(1, ch)
     lax.fori_loop(KB // 2, KB, compose, 0)
 
+    for n in (10, 11, 12):
+        loads[n].wait()
     def select_hot(i, carry):
         for h in range(2):
             cells = surface[pl.ds(2 * i + h, 1), :]
@@ -279,8 +290,6 @@
             for step in (1, 2, 3):
                 t_copy(step).start()
         sweep(1, ch, v1, v2)
-    out_copy = pltpu.make_async_copy(v2, vol_hbm, out_sem.at[0])
-    out_copy.start()
 
     def pick_box(i, carry):
         got = dot(a_sel[...], oh_sel[i])
@@ -435,6 +444,7 @@
     pl.when(has[2])(sides[1][1].wait_recv)
     for sent, c in sides:
         pl.when(sent)(c.wait_send)
+    loads[13].wait()
     base = me * 16 - 16
     for s in range(4):
         for b in range(16):
@@ -443,7 +453,6 @@
     force[...] = dot(pick[...], nblk[...].reshape(1024, 256))
 
     own_back.wait()
-    out_copy.wait()
 
     def bring(i, carry):
         kb = block_at(i)
@@ -471,6 +480,17 @@
     forcing[...] = force[...]
 
 
+def put_out(volume, forcing, volume_hbm, forcing_hbm, sem):
+    copies = [
+        pltpu.make_async_copy(volume, volume_hbm, sem.at[0]),
+        pltpu.make_async_copy(forcing, forcing_hbm, sem.at[1]),
+    ]
+    for c in copies:
+        c.start()
+    for c in copies:
+        c.wait()
+
+
 def shards(
     volume_field, source, material, mat_real, mat_loss, surface_map, near_boxes, near_blocks, radiate, interp,
     phase_angle, far_parents, far_kind, translate,
@@ -478,17 +498,18 @@
     shape = volume_field.shape
     any_ = pl.BlockSpec(memory_space=pl.ANY)
     vmem = pl.BlockSpec(memory_space=pltpu.VMEM)
-    smem = pl.BlockSpec(memory_space=pltpu.SMEM)
     V = pltpu.VMEM
     dma = pltpu.SemaphoreType.DMA
     volume, forcing = pl.pallas_call(
         kernel,
-        out_shape=(jax.ShapeDtypeStruct((2048, 128), f32), jax.ShapeDtypeStruct((256, 256), f32)),
-        in_specs=[any_, any_, vmem, smem, smem, vmem, smem, any_, any_, any_, vmem, vmem, vmem, any_],
-        out_specs=(any_, vmem),
+        out_shape=(pltpu.VMEM((2048, 128), f32), pltpu.VMEM((256, 256), f32)),
+        in_specs=[pl.BlockSpec(memory_space=pltpu.HBM)] * 14,
+        out_specs=(vmem, vmem),
         scratch_shapes=[
-            V((2048, 128), f32), V((2048, 128), f32), V((2048, 128), f32), V((2048, 128), f32),
+            V((2048, 128), f32), V((2048, 128), f32), V((2048, 128), f32),
             V((512, 2048), bf16), V((2, 128, 512), bf16), V((4, 256, 256), bf16), V((2, 32, 316), f32),
+            V((4, 16, 128), i32), pltpu.SMEM((8,), f32), pltpu.SMEM((8,), f32), V((16, 128), i32), pltpu.SMEM((4, 16), i32),
+            V((8, 2048), f32), V((8, 512), i32), V((8, 512), i32),
             V((64, 128), f32), V((64, 128), f32), V((64, 128), f32),
             V((2, 2, CHUNKS, 32 * PER, 128), bf16), V((2, 2, CHUNKS, 8 * PER, 128), bf16),
             V((2, 2, CHUNKS, 32 * PER, 128), bf16), V((2, 2, CHUNKS, 8 * PER, 128), bf16), V((2, 8 * PER, 128), f32),
@@ -498,16 +519,25 @@
             V((2, 128, KINDS_PAD), bf16), V((KINDS_PAD, 256), bf16), V((8, 512, 256), f32),
             V((64, 128), f32), V((64, 16, 128), bf16), V((1024, 128), bf16), V((512, 256), bf16),
             V((128, 128), f32), V((64, 16, 128), bf16), V((1024, 128), bf16), V((256, 256), bf16), V((256, 256), f32),
-            dma((6,)), dma((2, CHUNKS, 4)), dma((2, CHUNKS, 4)), dma((3,)), dma((3,)), dma((2,)), dma((2,)),
-            dma((1,)), dma((1,)), dma((1,)), dma((KB,)), dma((2,)), dma((1,)),
+            dma((14,)), dma((2, CHUNKS, 4)), dma((2, CHUNKS, 4)), dma((3,)), dma((3,)), dma((2,)), dma((2,)),
+            dma((1,)), dma((1,)), dma((1,)), dma((KB,)), dma((2,)),
             pltpu.SemaphoreType.REGULAR, pltpu.SemaphoreType.REGULAR,
         ],
-        compiler_params=pltpu.CompilerParams(collective_id=3, has_side_effects=True),
+        compiler_params=pltpu.CompilerParams(collective_id=3, has_side_effects=True, vmem_limit_bytes=VMEM_A),
         name="relax_and_couple",
     )(
         volume_field.reshape(2048, 128), source.reshape(2048, 128), material, mat_real, mat_loss, surface_map,
         near_boxes.T, near_blocks, radiate, interp, phase_angle, far_parents.T, far_kind.T, translate.transpose(1, 2, 0),
     )
+    volume, forcing = pl.pallas_call(
+        put_out,
+        out_shape=(jax.ShapeDtypeStruct((2048, 128), f32), jax.ShapeDtypeStruct((256, 256), f32)),
+        in_specs=[vmem, vmem],
+        out_specs=(any_, any_),
+        scratch_shapes=[dma((2,))],
+        compiler_params=pltpu.CompilerParams(vmem_limit_bytes=4 * 1024 * 1024),
+        name="put_out",
+    )(volume, forcing)
     return volume.reshape(shape), forcing.reshape(16, 16, 256)
 
 

time: 52.3 us -> 49.1 us (0.939)
  local copies, waits for them, and re-layouts: 3.06 us -> 0 us
    unnamed x4 -> x0, local copies, waits for them, and re-layouts: 3.06 us -> none
    pallas_call x1 -> x2, Pallas kernels: 48.4 us -> 48.3 us  [the longest x1 47.3 us: shards(): pl.pallas_call(kernel, out_shape=(pltpu.VMEM((2048, 128), f32), pltpu.VME...]
where the time goes in v4:
time: 49.1 us; the launch traced here: 49 us
  Pallas kernels  48.3 us (98%)
  between operations  0.64 us (1%)
    pallas_call x1, Pallas kernels, shards(): pl.pallas_call(kernel, out_shape=(pltpu.VMEM((2048, 128), f32), pltpu.VME...  47.3 us
    pallas_call x1, Pallas kernels, shards(): pl.pallas_call(put_out, out_shape=(jax.ShapeDtypeStruct((2048, 128), f32)...  1.07 us

profile of v4, /device:TPU:1, one launch (start us, length us, event | category | flops | bytes accessed | tf_op | source)
XLA Modules:
  0.0 49.0 jit_solution(8618978426215692638)
XLA Ops:
  0.6 47.3 %relax_and_couple.1 = (f32[2048,128]{1,0:T(8,128)S(1)}, f32[256,256]{1,0:T(8,128)S(1)}) custom-call(f32[2048,128]{1,0:T(8,128)} %bitcast.8, f32[2048,128]{1,0:T(8,128)} %bitcast.9, s32[4,16,128]{2,1,0:T(8,128)} %material_hbm.1, f32[8]{0:T(128)} %real_hbm.1, f32[8]{0:T(128)} %loss_hbm.1, s32[16,128]{1,0:T(8,128)} %surface_hbm.1, s32[4,16]{1,0:T(4,128)} %bitcast.13, ...), custom_call_target="tpu_custom_call" | custom-call | tf_op jit(solution)/shard_map/relax_and_couple/pallas_call | solution.py:503
  47.9 1.1 %put_out.1 = (f32[2048,128]{1,0:T(8,128)}, f32[256,256]{1,0:T(8,128)}) custom-call(f32[2048,128]{1,0:T(8,128)S(1)} %get-tuple-element.6.volume, f32[256,256]{1,0:T(8,128)S(1)} %get-tuple-element.7.forcing), custom_call_target="tpu_custom_call" | custom-call | tf_op jit(solution)/shard_map/put_out/pallas_call | solution.py:532

commit v5 on v4

--- a/solution.py
+++ b/solution.py
@@ -53,7 +53,7 @@
     p_col, k_col, oh_far, tt, tt_t, tg,
     frows, pb, g, gg, i2f, i2b, r, left, force,
     in_sem, halo_send, halo_recv, t_send, t_recv, near_send, near_recv, a_send, a_recv, back_send, back_recv,
-    self_sem, line_sem, all_sem,
+    self_sem, rounds,
 ):
     space = lax.axis_index("space")
     shard = lax.axis_index("shard")
@@ -84,7 +84,9 @@
         pl.semaphore_signal(sem, inc=1, device_id=to, device_id_type=MESH)
 
     x_line = [(space, lax.rem(at_x + k, 4) * 16 + at_z * 2 + at_y) for k in range(1, 4)]
-    z_line = [(space, at_x * 16 + lax.rem(at_z + k, 8) * 2 + at_y) for k in range(1, 8)]
+    def along_z(k):
+        return (space, at_x * 16 + lax.rem(at_z + k, 8) * 2 + at_y)
+
     y_group = [
         (lax.rem(space + s, 4), at_x * 16 + at_z * 2 + lax.rem(at_y + y, 2))
         for s in range(4)
@@ -92,7 +94,7 @@
         if s or y
     ]
     barrier = pltpu.get_barrier_semaphore()
-    for to in x_line + z_line + y_group + [(space, my_kb * 4 + 3 - my_j)]:
+    for to in x_line + [along_z(1), along_z(7)] + y_group + [(space, my_kb * 4 + 3 - my_j)]:
         signal(barrier, to)
 
     @pl.when(has_hop)
@@ -186,11 +188,17 @@
             pl.when(has[k ^ 1])(c.wait_recv)
             pl.when(has[k])(c.wait_send)
 
-    pl.semaphore_wait(barrier, 18 + has_hop.astype(i32))
+    pl.semaphore_wait(barrier, 13 + has_hop.astype(i32))
     for ch in range(CHUNKS):
         start_halo(0, ch)
-    for to in x_line:
-        signal(line_sem, to)
+    def round_out(n):
+        for to in ([along_z(1), along_z(7)], [along_z(2), along_z(6)], [along_z(4)], x_line)[n]:
+            signal(rounds.at[n], to)
+
+    def round_in(n):
+        pl.semaphore_wait(rounds.at[n], (2, 2, 1, 3)[n])
+
+    round_out(0)
 
     loads[1].wait()
     loads[2].wait()
@@ -212,9 +220,8 @@
         return carry
 
     lax.fori_loop(0, KB // 2, compose, 0)
-    pl.semaphore_wait(line_sem, 3)
-    for to in z_line:
-        signal(all_sem, to)
+    round_in(0)
+    round_out(1)
 
     def sweep(w, ch, old, new):
         for side in range(2):
@@ -257,7 +264,13 @@
         sweep(0, ch, v0, v1)
         faces_y(1, ch, v1)
         start_halo(1, ch)
+        if ch == CHUNKS // 2 - 1:
+            round_in(1)
+            round_out(2)
     lax.fori_loop(KB // 2, KB, compose, 0)
+
+    round_in(2)
+    round_out(3)
 
     for n in (10, 11, 12):
         loads[n].wait()
@@ -344,7 +357,7 @@
             ).start()
 
     pattern(0)
-    pl.semaphore_wait(all_sem, 7)
+    round_in(3)
 
     def step_out(i, carry):
         send_pattern(i - 1, 16)
@@ -521,7 +534,7 @@
             V((128, 128), f32), V((64, 16, 128), bf16), V((1024, 128), bf16), V((256, 256), bf16), V((256, 256), f32),
             dma((14,)), dma((2, CHUNKS, 4)), dma((2, CHUNKS, 4)), dma((3,)), dma((3,)), dma((2,)), dma((2,)),
             dma((1,)), dma((1,)), dma((1,)), dma((KB,)), dma((2,)),
-            pltpu.SemaphoreType.REGULAR, pltpu.SemaphoreType.REGULAR,
+            pltpu.SemaphoreType.REGULAR((4,)),
         ],
         compiler_params=pltpu.CompilerParams(collective_id=3, has_side_effects=True, vmem_limit_bytes=VMEM_A),
         name="relax_and_couple",

time: 49.1 us -> 49.1 us (level)
  no operation moved by 1% of the time
where the time goes in v5:
time: 49.1 us; the launch traced here: 49 us
  Pallas kernels  48.3 us (98%)
  between operations  0.64 us (1%)
    pallas_call x1, Pallas kernels, shards(): pl.pallas_call(kernel, out_shape=(pltpu.VMEM((2048, 128), f32), pltpu.VME...  47.3 us
    pallas_call x1, Pallas kernels, shards(): pl.pallas_call(put_out, out_shape=(jax.ShapeDtypeStruct((2048, 128), f32)...  1.07 us

profile of v5, /device:TPU:1, one launch (start us, length us, event | category | flops | bytes accessed | tf_op | source)
XLA Modules:
  0.0 49.0 jit_solution(9883675467582559454)
XLA Ops:
  0.6 47.3 %relax_and_couple.1 = (f32[2048,128]{1,0:T(8,128)S(1)}, f32[256,256]{1,0:T(8,128)S(1)}) custom-call(f32[2048,128]{1,0:T(8,128)} %bitcast.8, f32[2048,128]{1,0:T(8,128)} %bitcast.9, s32[4,16,128]{2,1,0:T(8,128)} %material_hbm.1, f32[8]{0:T(128)} %real_hbm.1, f32[8]{0:T(128)} %loss_hbm.1, s32[16,128]{1,0:T(8,128)} %surface_hbm.1, s32[4,16]{1,0:T(4,128)} %bitcast.13, ...), custom_call_target="tpu_custom_call" | custom-call | tf_op jit(solution)/shard_map/relax_and_couple/pallas_call | solution.py:516
  47.9 1.1 %put_out.1 = (f32[2048,128]{1,0:T(8,128)}, f32[256,256]{1,0:T(8,128)}) custom-call(f32[2048,128]{1,0:T(8,128)S(1)} %get-tuple-element.6.volume, f32[256,256]{1,0:T(8,128)S(1)} %get-tuple-element.7.forcing), custom_call_target="tpu_custom_call" | custom-call | tf_op jit(solution)/shard_map/put_out/pallas_call | solution.py:545

commit v6 on v5

--- a/solution.py
+++ b/solution.py
@@ -356,6 +356,8 @@
                 pb.at[kb * 4 + q, quarter(j)], g.at[my_rows], a_send.at[0], a_recv.at[0], (q, kb * 4 + j)
             ).start()
 
+    for sent, c in near_copies():
+        pl.when(sent)(c.start)
     pattern(0)
     round_in(3)
 
@@ -370,8 +372,6 @@
     own = pltpu.make_async_copy(pb.at[my_kb * 4 + space, quarter(my_j)], g.at[my_rows], self_sem.at[0])
     own.start()
 
-    for sent, c in near_copies():
-        pl.when(sent)(c.start)
     def block_rows(col, rb):
         first = (rb // 4) * 64 + lax.rem(rb, 4) * 8
         at = [first + q * 128 + x * 32 for q in range(SPACE) for x in range(2)]

time: 49.1 us -> 50.4 us (1.026)
  Pallas kernels: 48.3 us -> 49.7 us
    pallas_call x1, Pallas kernels: 47.3 us -> 48.6 us  [shards(): pl.pallas_call(kernel, out_shape=(pltpu.VMEM((2048, 128), f32), pltpu.VME...]
where the time goes in v6:
time: 50.4 us; the launch traced here: 50.3 us
  Pallas kernels  49.7 us (99%)
  between operations  0.64 us (1%)
    pallas_call x1, Pallas kernels, shards(): pl.pallas_call(kernel, out_shape=(pltpu.VMEM((2048, 128), f32), pltpu.VME...  48.6 us
    pallas_call x1, Pallas kernels, shards(): pl.pallas_call(put_out, out_shape=(jax.ShapeDtypeStruct((2048, 128), f32)...  1.07 us

profile of v6, /device:TPU:1, one launch (start us, length us, event | category | flops | bytes accessed | tf_op | source)
XLA Modules:
  0.0 50.3 jit_solution(10732941400788591022)
XLA Ops:
  0.6 48.6 %relax_and_couple.1 = (f32[2048,128]{1,0:T(8,128)S(1)}, f32[256,256]{1,0:T(8,128)S(1)}) custom-call(f32[2048,128]{1,0:T(8,128)} %bitcast.8, f32[2048,128]{1,0:T(8,128)} %bitcast.9, s32[4,16,128]{2,1,0:T(8,128)} %material_hbm.1, f32[8]{0:T(128)} %real_hbm.1, f32[8]{0:T(128)} %loss_hbm.1, s32[16,128]{1,0:T(8,128)} %surface_hbm.1, s32[4,16]{1,0:T(4,128)} %bitcast.13, ...), custom_call_target="tpu_custom_call" | custom-call | tf_op jit(solution)/shard_map/relax_and_couple/pallas_call | solution.py:516
  49.3 1.1 %put_out.1 = (f32[2048,128]{1,0:T(8,128)}, f32[256,256]{1,0:T(8,128)}) custom-call(f32[2048,128]{1,0:T(8,128)S(1)} %get-tuple-element.6.volume, f32[256,256]{1,0:T(8,128)S(1)} %get-tuple-element.7.forcing), custom_call_target="tpu_custom_call" | custom-call | tf_op jit(solution)/shard_map/put_out/pallas_call | solution.py:545
